TPU v7x, 32 devices: a whole 2x2x4 slice. The times are simulated.
32 devices in a mesh: parts: 2 (over y), tm: 4 (over z), sub: 2 (over x), inner: 2 (over core).
Axes of the slice: x: 2, y: 2, z: 4, core: 2. Of those that a mesh axis runs over, the one named last changes fastest.
Arguments:
- guess: float32 [512, 128], P(('parts', 'tm', 'sub', 'inner')), parts along dimension 0, may hold values from -6 to 6
- start: float32 [256], P('parts'), parts along dimension 0, may hold values from -6 to 6
- layer_weight: float32 [256, 64], replicated, may hold values from -0.75 to 0.75
- layer_bias: float32 [256], replicated, may hold values from -4 to 4
- amplitude: float32 [256], replicated, may hold values from 0.5 to 4
Outputs:
- updated: float32 [512, 128], P(('parts', 'tm', 'sub', 'inner')), parts along dimension 0
There are 2 independent parts, one for each index of `parts`. A program takes and returns all parts, laid end to end along the dimension named above; an argument that names none is the same for every part. Nothing has to cross between parts.
All inputs are finite; a program needn't handle non-finite values.
Results may differ from a plain program's by a relative error of at most 0.0003.
Values sent between devices are 32-bit elements; how exact they have to be, the bound alone decides.
No kernel may reach another device: no remote copies, remote signals or barrier semaphores. Data moves between devices by JAX's collectives and lax.ppermute only.
A program may use at most 128 MiB of HBM per device.

v0:
```python
import jax
import jax.numpy as jnp
from jax import lax
from jax.sharding import PartitionSpec as P

step_size = 0.04
curvature = 0.5


def from_behind(value, axis, steps):
    count = lax.axis_size(axis)
    first, last = (max(0, -steps), min(count, count - steps))
    return lax.ppermute(value, axis, [(source, source + steps) for source in range(first, last)])


def carried_in(value, axis, join, neutral):
    count, mine = (lax.axis_size(axis), lax.axis_index(axis))
    pieces = jax.tree.map(lambda part: lax.all_gather(part, axis), value)
    running = jax.tree.map(
        lambda part, zero: jnp.full_like(part, 0) + jnp.asarray(zero, part.dtype), value, neutral
    )

    def turn(position, running):
        longer = join(running, jax.tree.map(lambda part: part[position], pieces))
        return jax.tree.map(lambda new, old: jnp.where(position < mine, new, old), longer, running)

    return lax.fori_loop(0, count - 1, turn, running)


def broadcast(shard, axis, root):
    mine = lax.axis_index(axis) == root
    return lax.psum(jnp.where(mine, shard, jnp.zeros_like(shard)), axis)


def forces(coords, layer_weight, layer_bias, amplitude):
    hi = lax.Precision.HIGHEST
    pre = jnp.dot(coords, layer_weight.T, precision=hi) + layer_bias
    gate = jax.nn.sigmoid(pre)
    grad = jnp.dot(amplitude * gate, layer_weight, precision=hi) + curvature * coords
    return (grad, amplitude * gate * (1.0 - gate))


def hess_apply(vector, layer_weight, weights_d):
    hi = lax.Precision.HIGHEST
    inner_vals = jnp.dot(layer_weight, vector, precision=hi) * weights_d
    return jnp.dot(inner_vals, layer_weight, precision=hi) + curvature * vector


def hessian(layer_weight, weights_d):
    hi = lax.Precision.HIGHEST
    width = layer_weight.shape[1]
    scaled = layer_weight * weights_d[:, None]
    return jnp.dot(scaled.T, layer_weight, precision=hi) + curvature * jnp.eye(
        width, dtype=jnp.float32
    )


def combine(earlier, later):
    hi = lax.Precision.HIGHEST
    map_early, shift_early = earlier
    map_late, shift_late = later
    return (
        jnp.dot(map_late, map_early, precision=hi),
        jnp.dot(map_late, shift_early, precision=hi) + shift_late,
    )


def shards(guess, start, layer_weight, layer_bias, amplitude):
    hi = lax.Precision.HIGHEST
    width = layer_weight.shape[1]
    state_len = 2 * width
    received = from_behind(guess[-1], ("tm", "sub", "inner"), 1)
    previous = jnp.where(lax.axis_index(("tm", "sub", "inner")) == 0, start, received)
    before = jnp.concatenate([previous[None, :], guess[:-1]], axis=0)
    coords, momenta = (before[:, :width], before[:, width:])
    grad_zero, curve_zero = forces(coords, layer_weight, layer_bias, amplitude)
    half = momenta - 0.5 * step_size * grad_zero
    moved = coords + step_size * half
    grad_one, curve_one = forces(moved, layer_weight, layer_bias, amplitude)
    landed = half - 0.5 * step_size * grad_one
    image = jnp.concatenate([moved, landed], axis=1)
    unit = jnp.eye(width, dtype=jnp.float32)

    def compose(carry, items):
        window_map, window_shift = carry
        prior, curve_a, curve_b, target = items
        hess_a = hessian(layer_weight, curve_a)
        hess_b = hessian(layer_weight, curve_b)
        block_qq = unit - 0.5 * step_size * step_size * hess_a
        block_pq = -0.5 * step_size * (hess_a + jnp.dot(hess_b, block_qq, precision=hi))
        block_pp = unit - 0.5 * step_size * step_size * hess_b
        jacobian = jnp.block([[block_qq, step_size * unit], [block_pq, block_pp]])
        offset = target - jnp.dot(jacobian, prior, precision=hi)
        new_map = jnp.dot(jacobian, window_map, precision=hi)
        new_shift = jnp.dot(jacobian, window_shift, precision=hi) + offset
        return ((new_map, new_shift), None)

    identity = (jnp.eye(state_len, dtype=jnp.float32), jnp.zeros((state_len,), jnp.float32))
    local, unused = lax.scan(compose, identity, (before, curve_zero, curve_one, image))
    lower = carried_in(local, ("sub", "inner"), combine, identity)
    closing = combine(lower, local)
    total = (
        broadcast(closing[0], ("sub", "inner"), lax.axis_size(("sub", "inner")) - 1),
        broadcast(closing[1], ("sub", "inner"), lax.axis_size(("sub", "inner")) - 1),
    )
    major = carried_in(total, "tm", combine, identity)
    prefix = combine(major, lower)
    entering = jnp.dot(prefix[0], start, precision=hi) + prefix[1]

    def advance(state, items):
        prior, curve_a, curve_b, target = items
        delta = state - prior
        delta_q, delta_p = (delta[:width], delta[width:])
        first = hess_apply(delta_q, layer_weight, curve_a)
        new_q = delta_q - 0.5 * step_size * step_size * first + step_size * delta_p
        new_p = (
            delta_p
            - 0.5 * step_size * first
            - 0.5 * step_size * hess_apply(new_q, layer_weight, curve_b)
        )
        result = target + jnp.concatenate([new_q, new_p])
        return (result, result)

    final, states = lax.scan(advance, entering, (before, curve_zero, curve_one, image))
    return states


def solution(mesh):
    placed = (P(("parts", "tm", "sub", "inner"), None), P("parts"), P(), P(), P())
    return jax.shard_map(
        shards,
        mesh=mesh,
        in_specs=placed,
        out_specs=P(("parts", "tm", "sub", "inner"), None),
        check_vma=False,
    )
```

profile of v0, /device:TPU:0, one launch (start us, length us, event | category | flops | bytes accessed | tf_op | source)
XLA Modules:
  0.0 143.9 jit_solution(9281563523348621520)
XLA Ops:
  7.2 2.4 %collective-permute-start = (f32[128]{0:T(128)S(1)}, f32[128]{0:T(128)S(1)}, u32[]{:S(2)}, u32[]{:S(2)}) collective-permute-start(f32[128]{0:T(128)S(1)} %slice_bitcast_fusion), channel_id=1, source_target_pairs={{0,1},{1,2},{2,3},{3,4},{4,5},{5,6},{6,7},{7,8},{8,9},{9,10},{10,1... | collective-permute-start | bytes 1544 | tf_op jit(solution)/shard_map/ppermute | solution.py:13
  13.5 24.4 %while.61 = (s32[]{:T(128)}, f32[128,128]{1,0:T(8,128)S(1)}, f32[128]{0:T(128)S(1)}, f32[16,256]{1,0:T(8,128)S(1)}, f32[256,64]{0,1:T(8,128)S(1)}, /*index=5*/f3...) while((s32[]{:T(128)}, f32[128,128]{1,0:T(8,128)S(1)}, ...), condition=%wide.region_1.2_spmd.clone.clone, body=%wide.region_0.1_spmd.clone.clone.sunk | while | flops 54133120 | bytes 797811 | solution.py:99
  37.9 8.5 %all-gather = f32[512,128]{1,0:T(8,128)S(1)} all-gather(f32[128,128]{1,0:T(8,128)S(1)} %get-tuple-element.321), channel_id=2, replica_groups=mesh['parts'=2,'tm'=4,'sub'=2,'inner'=2] {'sub','inner'}, dimensions={0}, use_global_device_ids=true | all-gather | bytes 327680 | tf_op jit(solution)/shard_map/all_gather | solution.py:18
  46.4 5.0 %all-gather.2 = f32[4,1,128]{2,1,0:T(1,128)S(1)} all-gather(f32[1,1,128]{2,1,0:T(1,128)S(1)} %bitcast.249), channel_id=3, replica_groups=mesh['parts'=2,'tm'=4,'sub'=2,'inner'=2] {'sub','inner'}, dimensions={0}, use_global_device_ids=true | all-gather | bytes 2560 | tf_op jit(solution)/shard_map/all_gather | solution.py:18
  51.4 1.4 while.59
  53.9 7.1 %psum.15 = f32[1,128]{1,0:T(1,128)S(1)} all-reduce(f32[1,128]{1,0:T(1,128)S(1)} %fusion.68), channel_id=1, replica_groups=mesh['parts'=2,'tm'=4,'sub'=2,'inner'=2] {'sub','inner'}, use_global_device_ids=true, to_apply=%region_5.6 | all-reduce | flops 128 | bytes 1024 | tf_op jit(solution)/shard_map/psum | solution.py:32
  61.1 11.1 %all-gather.3 = f32[4,1,128]{2,1,0:T(1,128)S(1)} all-gather(f32[1,1,128]{2,1,0:T(1,128)S(1)} %bitcast.250), channel_id=1, replica_groups=mesh['parts'=2,'tm'=4,'sub'=2,'inner'=2] {'tm'}, dimensions={0}, use_global_device_ids=true | all-gather | bytes 2560 | tf_op jit(solution)/shard_map/all_gather | solution.py:18
  72.2 14.5 %all-reduce.2.cloned.1.call-done = f32[1,128,128]{2,1,0:T(8,128)} async-done(((f32[1,128,128]{2,1,0:T(8,128)}), f32[1,128,128]{2,1,0:T(8,128)}) %all-reduce.2.cloned.1.call-update) | async-done | bytes 65552 | tf_op jit(solution)/shard_map/psum | solution.py:32
  86.7 14.1 %all_gather.29 = f32[4,128,128]{2,1,0:T(8,128)S(1)} all-gather(f32[1,128,128]{2,1,0:T(8,128)} %all-reduce.2.cloned.1.call-done), channel_id=1, replica_groups=mesh['parts'=2,'tm'=4,'sub'=2,'inner'=2] {'tm'}, dimensions={0}, use_global_device_ids=true | all-gather | bytes 327680 | tf_op jit(solution)/shard_map/all_gather | solution.py:18
  100.8 1.4 while.60
  102.8 34.2 %while.58 = (s32[]{:T(128)}, f32[128]{0:T(128)S(1)}, f32[16,128]{1,0:T(8,128)}, f32[16,128]{1,0:T(8,128)S(1)}, f32[16,128]{1,0:T(8,128)S(1)}, /*index=5*/f32[256...) while((s32[]{:T(128)}, f32[128]{0:T(128)S(1)}, ...), condition=%wide.region_9.10_spmd, body=%wide.region_8.9_spmd.sunk | while | flops 788354 | bytes 285049 | solution.py:124
  103.6 1.3 dynamic_update_slice.5
  105.8 1.3 dynamic_update_slice.5
  107.9 1.3 dynamic_update_slice.5
  110.0 1.3 dynamic_update_slice.5
  112.2 1.3 dynamic_update_slice.5
  114.3 1.3 dynamic_update_slice.5
  116.5 1.3 dynamic_update_slice.5
  118.6 1.3 dynamic_update_slice.5
  120.7 1.3 dynamic_update_slice.5
  122.9 1.3 dynamic_update_slice.5
  125.0 1.3 dynamic_update_slice.5
  127.1 1.3 dynamic_update_slice.5
  129.3 1.3 dynamic_update_slice.5
  (389 shorter events, 49.1 us)
Async XLA Ops:
  6.5 80.2 %all-reduce.2.cloned.1.call-start = ((), (), s32[]{:S(2)}) async-start(), calls=%async_computation | async-start | bytes 131072 | tf_op jit(solution)/shard_map/psum | solution.py:32
  7.2 3.2 %collective-permute-start = (f32[128]{0:T(128)S(1)}, f32[128]{0:T(128)S(1)}, u32[]{:S(2)}, u32[]{:S(2)}) collective-permute-start(f32[128]{0:T(128)S(1)} %slice_bitcast_fusion), channel_id=1, source_target_pairs={{0,1},{1,2},{2,3},{3,4},{4,5},{5,6},{6,7},{7,8},{8,9},{9,10},{10,1... | collective-permute-start | bytes 1544 | tf_op jit(solution)/shard_map/ppermute | solution.py:13
  9.6 0.6 copy-start.1
  10.3 0.8 copy-start
  10.3 0.8 copy-start.7
  10.3 0.7 copy-start.10
  11.0 0.7 copy-start.9
  11.7 0.7 copy-start.8
  12.7 0.8 copy-start.5
  37.9 13.6 %copy-start.6 = (f32[128,128]{1,0:T(8,128)S(1)}, f32[128,128]{1,0:T(8,128)}, u32[]{:S(2)}) copy-start(f32[128,128]{1,0:T(8,128)} %copy-done.1) | copy-start | bytes 196612
  52.9 0.8 copy-start.3
  72.2 28.5 %copy-start.2 = (f32[128,128]{1,0:T(8,128)S(1)}, f32[128,128]{1,0:T(8,128)}, u32[]{:S(2)}) copy-start(f32[128,128]{1,0:T(8,128)} %copy-done.1) | copy-start | bytes 196612
  100.8 1.4 %copy-start.4 = (f32[128,128]{1,0:T(8,128)S(1)}, f32[128,128]{1,0:T(8,128)}, u32[]{:S(2)}) copy-start(f32[128,128]{1,0:T(8,128)} %copy-done.3) | copy-start | bytes 196612
Sparse Core Ops, SparseCore 0:
  53.9 32.7 all-reduce.1
where the time goes:
time: 145 us; the launch traced here: 144 us
  blocking collectives  45.9 us (32%)
  matrix products  36.6 us (25%)
  local copies, waits for them, and re-layouts  25.9 us (18%)
  waiting for transfers between devices  14.6 us (10%)
  between operations  13.5 us (9%)
  other arithmetic  3.46 us (2%)
  starting transfers between devices  2.39 us (2%)
  loops' own time  1.58 us (1%)
    all_gather x4, blocking collectives, carried_in(): pieces = jax.tree.map(lambda part: lax.all_gather(part, axis), value)  38.7 us
    dynamic_update_slice x16, local copies, waits for them, and re-layouts, shards(): lax.scan(advance, entering, (before, curve_zero, curve_one, image))  20.8 us
    psum x1, waiting for transfers between devices, broadcast(): return lax.psum(jnp.where(mine, shard, jnp.zeros_like(shard)), axis)  14.5 us
    psum x1, blocking collectives, broadcast(): return lax.psum(jnp.where(mine, shard, jnp.zeros_like(shard)), axis)  7.14 us
    dot_general x32, matrix products, hessian(): jnp.dot(scaled.T, layer_weight, precision=hi)  6.57 us
    dot_general x32, matrix products, hess_apply(): inner_vals = jnp.dot(layer_weight, vector, precision=hi) * weights_d  4.9 us
    dot_general x32, matrix products, hess_apply(): return jnp.dot(inner_vals, layer_weight, precision=hi) + curvature * vector  4.78 us
    dot_general x16, matrix products, compose(): new_shift = jnp.dot(jacobian, window_shift, precision=hi) + offset  4.76 us
  transfers between devices with their start and end apart: 2, of which 2 were waited for; matrix products, arithmetic and copies ran while one was open for 0% of the time, Pallas kernels for 0%

commit v1 on v0

v1 whole, which is shorter than its diff:
```python
import functools
import jax
import jax.numpy as jnp
from jax import lax
from jax.experimental import pallas as pl
from jax.experimental.pallas import tpu as pltpu
from jax.sharding import PartitionSpec as P

step_size = 0.04
curvature = 0.5
PAD = 16

NN = (((1,), (0,)), ((), ()))
NT = (((1,), (1,)), ((), ()))


def split(value):
    high = value.astype(jnp.bfloat16)
    return high, (value - high.astype(jnp.float32)).astype(jnp.bfloat16)


def dot3(left, right, dims=NN):
    (left_high, left_low), (right_high, right_low) = left, right
    one = functools.partial(lax.dot_general, dimension_numbers=dims, preferred_element_type=jnp.float32)
    return one(left_high, right_high) + (one(left_high, right_low) + one(left_low, right_high))


def join(early, late):
    state = late.shape[1]
    product = dot3(split(early), split(late[:state]))
    return jnp.concatenate([product[:state], product[state:] + late[state:]], axis=0)


def local_kernel(guess_ref, start_ref, weight_ref, bias_ref, amp_ref,
                 total_ref, first_ref, tree_ref, kicks_ref, kick_first_ref, shifts_ref, curve_ref):
    rows, state = guess_ref.shape
    width = state // 2
    h = step_size
    guess = guess_ref[...]
    points = jnp.concatenate([guess, jnp.broadcast_to(start_ref[...], (8, state))], axis=0)
    weight = weight_ref[...]
    weight2 = split(weight)
    bias, amp = bias_ref[...], amp_ref[...]
    coords, momenta = points[:, :width], points[:, width:]

    def forces(at):
        gate = jax.nn.sigmoid(dot3(split(at), weight2) + bias)
        scaled = amp * gate
        grad = dot3(split(scaled), weight2, NT) + curvature * at
        return grad, scaled * (1.0 - gate)

    grad_zero, curve_zero = forces(coords)
    half = momenta - 0.5 * h * grad_zero
    moved = coords + h * half
    grad_one, curve_one = forces(moved)
    landed = half - 0.5 * h * grad_one
    image = jnp.concatenate([moved, landed], axis=1)
    first_ref[...] = image[rows:]

    residual = image[:rows - 1] - guess[1:]
    residual = jnp.concatenate([residual, jnp.zeros((1, state), jnp.float32)], axis=0)
    curve_next = jnp.concatenate([curve_zero[1:rows], jnp.zeros((1, curve_zero.shape[1]), jnp.float32)], axis=0)
    pushed = residual[:, :width]
    inner = dot3(split(pushed), weight2) * curve_next
    kicked = 0.5 * h * (dot3(split(inner), weight2, NT) + curvature * pushed)
    shifts = jnp.concatenate([pushed, residual[:, width:] - kicked], axis=1)
    row_id = lax.broadcasted_iota(jnp.int32, (rows, state), 0)
    shifts = jnp.where(row_id == rows - 1, image[:rows], shifts)
    shifts_ref[...] = shifts
    curve_ref[...] = curve_zero[:rows]

    double = jnp.concatenate([weight, weight], axis=0)
    double2 = split(double)
    line = lax.broadcasted_iota(jnp.int32, (width, state), 0)
    lane = lax.broadcasted_iota(jnp.int32, (width, state), 1)
    unit2 = jnp.where((lane == line) | (lane == line + width), 1.0, 0.0)
    right = lane >= width
    unit_top = jnp.where(lane == line, 1.0, 0.0)
    unit_low = jnp.where(lane == line + width, 1.0, 0.0)
    between = (curve_one[:rows] + curve_next) * (0.5 * h)

    def kick(weights_row, count):
        scaled = weight * weights_row
        return dot3(split(scaled), double2, NT) + (0.5 * h * curvature * count) * unit2

    kick_first = kick(curve_zero[0:1] * (0.5 * h), 1)
    kick_first_ref[...] = kick_first
    kicks = [kick(between[j:j + 1], 2 if j < rows - 1 else 1) for j in range(rows)]
    for j in range(0, rows, 2):
        kicks_ref[j // 2] = kicks[j]

    rolled = jnp.concatenate([shifts[:, width:], shifts[:, :width]], axis=1)
    lane_rows = lax.broadcasted_iota(jnp.int32, (rows, state), 1)
    drifted = shifts + jnp.where(lane_rows < width, h * rolled, 0.0)
    level = []
    for k in range(rows // 2):
        a, b = kicks[2 * k], kicks[2 * k + 1]
        moved_row = jnp.broadcast_to(drifted[2 * k:2 * k + 1, :width], (PAD, width))
        left = jnp.concatenate([a[:, :width], moved_row], axis=0)
        both = dot3(split(left), split(b))
        prod = both[:width]
        top = unit_top - jnp.where(right, a + b - h * prod, h * a)
        low = 2 * h * unit_top + unit_low - jnp.where(right, h * a + 2 * h * b - (h * h) * prod, (h * h) * a)
        if k == 0:
            top = top - dot3(split(kick_first[:, :width]), split(low))
        tail = drifted[2 * k:2 * k + 1] - jnp.where(right[:PAD], both[width:], 0.0) + shifts[2 * k + 1:2 * k + 2]
        level.append(jnp.concatenate([top, low, tail], axis=0))
    slot = 0
    while len(level) > 1:
        for item in level[::2]:
            tree_ref[slot] = item
            slot += 1
        level = [join(level[i], level[i + 1]) for i in range(0, len(level), 2)]
    total = level[0]
    total_ref[:state] = total[:state]
    tail_row = lax.broadcasted_iota(jnp.int32, (8, state), 0)
    total_ref[state:] = jnp.where(tail_row == 0, total[state:state + 8], jnp.broadcast_to(guess[0:1], (8, state)))


def spread(packed, state):
    return packed[:state], packed[state:state + 1], packed[state + 1:state + 2]


def apply(state_rows, packed):
    size = packed.shape[1]
    matrix, shift, origin = spread(packed, size)
    return dot3(split(state_rows - origin), split(matrix)) + shift


def compose(early, late):
    size = early.shape[1]
    matrix_a, shift_a, origin_a = spread(early, size)
    matrix_b, shift_b, origin_b = spread(late, size)
    left = jnp.concatenate([matrix_a, jnp.broadcast_to(shift_a - origin_b, (PAD, size))], axis=0)
    product = dot3(split(left), split(matrix_b))
    tail_row = lax.broadcasted_iota(jnp.int32, (8, size), 0)
    tail = jnp.where(tail_row == 0, product[size:size + 8] + shift_b, jnp.broadcast_to(origin_a, (8, size)))
    return jnp.concatenate([product[:size], tail], axis=0)


def ordered(own_ref, others, stack_ref, place, source):
    stack_ref[place] = own_ref[...]
    for index, other in enumerate(others):
        stack_ref[source(place, index + 1)] = other[...]


def total_kernel(source, axis_place, count, own_ref, *refs):
    others, (out_ref, stack_ref) = refs[:count - 1], refs[count - 1:]
    ordered(own_ref, others, stack_ref, axis_place(), source)
    total = stack_ref[0]
    for position in range(1, count):
        total = compose(total, stack_ref[position])
    out_ref[...] = total


def reach_kernel(source, axis_place, count, first_ref, own_ref, *refs):
    others, (out_ref, stack_ref) = refs[:count - 1], refs[count - 1:]
    ordered(own_ref, others, stack_ref, axis_place(), source)
    state = first_ref[...]
    for position in range(count):
        state = apply(state, stack_ref[position])
    out_ref[...] = state


def finish_kernel(groups, rows, entering_ref, guess_ref, weight_ref, tree_ref, kicks_ref, kick_first_ref,
                  shifts_ref, curve_ref, *refs):
    size = guess_ref.shape[1]
    width = size // 2
    h = step_size
    out_ref = refs[-1 - len(groups)]
    stacks = refs[len(refs) - len(groups):]
    state = entering_ref[...]
    used = 0
    for (source, axis_place, count), stack_ref in zip(groups, stacks):
        own_ref, others = refs[used], refs[used + 1:used + count]
        used += count
        place = axis_place()
        ordered(own_ref, others, stack_ref, place, source)
        state = lax.fori_loop(0, place, lambda i, s, stack_ref=stack_ref: apply(s, stack_ref[i]), state)
    guess = guess_ref[...]
    delta = state - guess[0:1]

    def go(vector, item):
        return dot3(split(vector), split(item[:size])) + item[size:size + 8]

    count = rows // 2
    sizes = []
    n = count
    while n > 1:
        sizes.append((n + 1) // 2)
        n //= 2
    starts = [sum(sizes[:i]) for i in range(len(sizes))]
    offsets = {0: delta}
    span = count
    for lev in reversed(range(len(sizes))):
        span //= 2
        for i in range(sizes[lev]):
            offsets[(2 * i + 1) * span] = go(offsets[2 * i * span], tree_ref[starts[lev] + i])

    left = lax.broadcasted_iota(jnp.int32, (8, size), 1) < width

    def kick(vector, matrix):
        moved = dot3(split(vector[:, :width]), split(matrix))
        return vector - jnp.where(left, 0.0, moved)

    def drift(vector):
        other = jnp.concatenate([vector[:, width:], vector[:, :width]], axis=1)
        return vector + jnp.where(left, h * other, 0.0)

    pieces = []
    for i in range(count):
        begin = offsets[i]
        if i > 0:
            pieces.append(begin[0:1])
        else:
            pieces.append(jnp.zeros((1, size), jnp.float32))
            begin = kick(begin, kick_first_ref[...])
        after = kick(drift(begin), kicks_ref[i]) + shifts_ref[2 * i:2 * i + 1]
        pieces.append(after[0:1])
    kicked = jnp.concatenate(pieces, axis=0)
    weight2 = split(weight_ref[...])
    pushed = kicked[:, :width]
    inner = dot3(split(pushed), weight2) * curve_ref[...]
    back = 0.5 * h * (dot3(split(inner), weight2, NT) + curvature * pushed)
    result = kicked + jnp.concatenate([jnp.zeros_like(back), back], axis=1) + guess
    row_id = lax.broadcasted_iota(jnp.int32, (rows, size), 0)
    out_ref[...] = jnp.where(row_id == 0, jnp.broadcast_to(state[0:1], (rows, size)), result)


def call(kernel, out_shape, scratch=(), flops=2_000_000, name=None):
    return pl.pallas_call(
        kernel,
        out_shape=out_shape,
        scratch_shapes=scratch,
        cost_estimate=pl.CostEstimate(flops=flops, bytes_accessed=200_000, transcendentals=0),
        name=name,
    )


def solution(mesh):
    parts, majors, subs, inners = (mesh.shape[name] for name in ("parts", "tm", "sub", "inner"))
    axes = ("tm", "sub", "inner")
    low = 2 if majors % 2 == 0 else 1
    blocks = majors // low
    group = low * subs

    def flat(block, place, inner):
        return (block * group + place) * inners + inner

    def partner(place, turn, count):
        return place ^ turn if count & (count - 1) == 0 else (place + turn) % count

    def origin(place, turn, count):
        return place ^ turn if count & (count - 1) == 0 else lax.rem(place - turn + count, count)

    def inner_place():
        return lax.axis_index("inner")

    def group_place():
        return lax.rem(lax.axis_index("tm"), low) * subs + lax.axis_index("sub")

    def shards(guess, start, layer_weight, layer_bias, amplitude):
        rows, size = guess.shape
        width, hidden = size // 2, layer_weight.shape[0]
        f32 = functools.partial(jax.ShapeDtypeStruct, dtype=jnp.float32)
        packed = f32((size + 8, size))
        weight_t = layer_weight.T
        nodes = rows // 2 - 1
        total, first, tree, kicks, kick_first, shifts, curve = call(
            local_kernel,
            [packed, f32((8, size)), f32((nodes, size + PAD, size)), f32((rows // 2, width, size)),
             f32((width, size)), f32((rows, size)), f32((rows, hidden))],
            name="local_maps", flops=100_000_000,
        )(guess, start[None, :], weight_t, layer_bias[None, :], amplitude[None, :])

        def exchange(value, pairs):
            return lax.ppermute(value, axes, pairs)

        inner_maps = [total]
        for turn in range(1, inners):
            inner_maps.append(exchange(total, [
                (flat(b, g, i), flat(b, g, partner(i, turn, inners)))
                for b in range(blocks) for g in range(group) for i in range(inners)]))
        inner_source = functools.partial(origin, count=inners)
        chip = total
        if inners > 1:
            chip = call(functools.partial(total_kernel, inner_source, inner_place, inners), packed,
                        [pltpu.VMEM((inners,) + packed.shape, jnp.float32)], name="chip_total")(*inner_maps)
        group_maps = [chip]
        for turn in range(1, group):
            group_maps.append(exchange(chip, [
                (flat(b, g, i), flat(b, partner(g, turn, group), (i + 1) % inners))
                for b in range(blocks) for g in range(group) for i in range(inners)]))
        group_source = functools.partial(origin, count=group)
        group_stack = [pltpu.VMEM((group,) + packed.shape, jnp.float32)]

        entering = first
        ahead = []
        if blocks > 1:
            block = lax.axis_index("tm") // low
            top = 1
            while top * 2 < blocks:
                top *= 2
            if blocks > 2:
                span = call(functools.partial(total_kernel, group_source, group_place, group), packed, group_stack,
                            name="block_total")(*group_maps)
            reach = None
            turn = 1
            while turn < top:
                arrived = exchange(span, [
                    (flat(b, g, i), flat((b ^ turn) % blocks if (b ^ turn) < blocks else b, g, (i + 1) % inners))
                    for b in range(blocks) for g in range(group) for i in range(inners)])
                upper = (block & turn) != 0
                known = (block ^ turn) < blocks
                early, late = jnp.where(upper, arrived, span), jnp.where(upper, span, arrived)
                joined = call(lambda a_ref, b_ref, o_ref: o_ref.__setitem__(..., compose(a_ref[...], b_ref[...])),
                              packed, name="span_total")(early, late)
                ahead.append((upper, arrived))
                span = jnp.where(known | upper, joined, span)
                turn *= 2
            if blocks == 2:
                reach = call(functools.partial(reach_kernel, group_source, group_place, group), f32((8, size)),
                             group_stack, name="block_reach")(first, *group_maps)
            else:
                reach = call(lambda f_ref, m_ref, o_ref: o_ref.__setitem__(..., apply(f_ref[...], m_ref[...])),
                             f32((8, size)), name="span_reach")(first, span)
            if blocks == 2 * top:
                pairs = [(flat(b, g, i), flat(b ^ top, g, (i + 1) % inners))
                         for b in range(blocks) for g in range(group) for i in range(inners)]
            else:
                pairs = [(flat(b, g, i), flat((b + top) % blocks, g, (i + 1) % inners))
                         for b in range(blocks) for g in range(group) for i in range(inners)]
            arrived = exchange(reach, pairs)
            entering = jnp.where(block >= top, arrived, first)
            for upper, value in reversed(ahead):
                moved = call(lambda f_ref, m_ref, o_ref: o_ref.__setitem__(..., apply(f_ref[...], m_ref[...])),
                             f32((8, size)), name="span_step")(entering, value)
                entering = jnp.where(upper, moved, entering)

        groups = []
        maps = []
        scratch = []
        if group > 1:
            groups.append((group_source, group_place, group))
            maps += group_maps
            scratch += group_stack
        if inners > 1:
            groups.append((inner_source, inner_place, inners))
            maps += inner_maps
            scratch.append(pltpu.VMEM((inners,) + packed.shape, jnp.float32))
        return call(functools.partial(finish_kernel, groups, rows), f32((rows, size)), scratch, name="finish")(
            entering, guess, weight_t, tree, kicks, kick_first, shifts, curve, *maps)

    placed = (P(("parts",) + axes, None), P("parts"), P(), P(), P())
    return jax.shard_map(
        shards,
        mesh=mesh,
        in_specs=placed,
        out_specs=P(("parts",) + axes, None),
        check_vma=False,
    )
```

time: 145 us -> 28.9 us (0.20)
  blocking collectives: 45.9 us -> 0 us
  matrix products: 36.6 us -> 0 us
  local copies, waits for them, and re-layouts: 25.9 us -> 1.25 us
  between operations: 13.5 us -> 0.01 us
  Pallas kernels: 0 us -> 11.7 us
  waiting for transfers between devices: 14.6 us -> 8.15 us
  starting transfers between devices: 2.39 us -> 6.97 us
  other arithmetic: 3.46 us -> 0.59 us
  loops' own time: 1.58 us -> 0 us
    all_gather x4 -> x0, blocking collectives: 38.7 us -> none  [carried_in(): pieces = jax.tree.map(lambda part: lax.all_gather(part, axis), value)]
    dot_general x181 -> x0, matrix products: 36.6 us -> none  [the longest x32 6.57 us: hessian(): jnp.dot(scaled.T, layer_weight, precision=hi)]
    dynamic_update_slice x16 -> x0, local copies, waits for them, and re-layouts: 20.8 us -> none  [shards(): lax.scan(advance, entering, (before, curve_zero, curve_one, image))]
    psum x1 -> x0, waiting for transfers between devices: 14.5 us -> none  [broadcast(): return lax.psum(jnp.where(mine, shard, jnp.zeros_like(shard)), axis)]
    pallas_call x0 -> x4, Pallas kernels: none -> 11.7 us  [the longest x1 4.73 us: shards(): call(local_kernel, [packed, f32((8, size)), f32((nodes, size + PAD, size)...]
    ppermute x1 -> x5, waiting for transfers between devices: 0.14 us -> 8.15 us  [exchange(): return lax.ppermute(value, axes, pairs)]
    psum x1 -> x0, blocking collectives: 7.14 us -> none  [broadcast(): return lax.psum(jnp.where(mine, shard, jnp.zeros_like(shard)), axis)]
    ppermute x1 -> x5, starting transfers between devices: 2.38 us -> 6.97 us  [exchange(): return lax.ppermute(value, axes, pairs)]
  transfers between devices with their start and end apart: 2 -> 5, of which waited for: 2 -> 5; matrix products, arithmetic and copies ran while one was open for 0% -> 0% of each run, Pallas kernels for 0% -> 0%
where the time goes in v1:
time: 28.9 us; the launch traced here: 28.7 us
  Pallas kernels  11.7 us (40%)
  waiting for transfers between devices  8.15 us (28%)
  starting transfers between devices  6.97 us (24%)
  local copies, waits for them, and re-layouts  1.25 us (4%)
  other arithmetic  0.59 us (2%)
    ppermute x5, waiting for transfers between devices, exchange(): return lax.ppermute(value, axes, pairs)  8.15 us
    ppermute x5, starting transfers between devices, exchange(): return lax.ppermute(value, axes, pairs)  6.97 us
    pallas_call x1, Pallas kernels, shards(): call(local_kernel, [packed, f32((8, size)), f32((nodes, size + PAD, size)...  4.73 us
    pallas_call x1, Pallas kernels, shards(): call(functools.partial(finish_kernel, groups, rows), f32((rows, size)), s...  3.01 us
    pallas_call x1, Pallas kernels, shards(): call(functools.partial(reach_kernel, group_source, group_place, group), f...  2.18 us
    pallas_call x1, Pallas kernels, shards(): call(functools.partial(total_kernel, inner_source, inner_place, inners),...  1.77 us
    unnamed x10, local copies, waits for them, and re-layouts  1.25 us
    select_n x1, other arithmetic, shards(): entering = jnp.where(block >= top, arrived, first)  0.59 us
  transfers between devices with their start and end apart: 5, of which 5 were waited for; matrix products, arithmetic and copies ran while one was open for 0% of the time, Pallas kernels for 0%

profile of v1, /device:TPU:0, one launch (start us, length us, event | category | flops | bytes accessed | tf_op | source)
XLA Modules:
  0.0 28.7 jit_solution(453849047757965977)
XLA Ops:
  0.0 4.7 %local_maps.1 = (f32[136,128]{1,0:T(8,128)}, f32[8,128]{1,0:T(8,128)}, f32[7,144,128]{2,1,0:T(8,128)}, f32[8,64,128]{2,1,0:T(8,128)}, f32[64,128]{1,0:T(8,128)}, /*index=5*/f32[16,128]{1,0:T(8,128)}, f32[16,256]{1,0:T(8,128)}) custom-call(f32[16,128]{1,0:T(8,128)} %guess_ref.3, f32[1,128]{1,0:T(1,128)} %bitcast.8, f32[64,256]{1,0:T(8,128)} %bitcast.4, ...), custom_call_target="tpu_custom_call" | custom-call | flops 100000000 | bytes 200000 | tf_op jit(solution)/shard_map/local_maps/pallas_call | solution.py:269
  4.7 0.5 %collective-permute-start = (f32[136,128]{1,0:T(8,128)}, f32[136,128]{1,0:T(8,128)S(1)}, u32[]{:S(2)}, u32[]{:S(2)}) collective-permute-start(f32[136,128]{1,0:T(8,128)} %get-tuple-element.13.own_ref.refs_4_), channel_id=1, source_target_pairs={{0,1},{1,0},{2,3},{3,2},{4,5},{5,4},{6,7},{7,6},{8,9},{9,8},{10,11... | collective-permute-start | bytes 208904 | tf_op jit(solution)/shard_map/ppermute | solution.py:277
  5.2 1.1 %collective-permute-done.refs_0_.refs_5_ = f32[136,128]{1,0:T(8,128)S(1)} collective-permute-done((f32[136,128]{1,0:T(8,128)}, f32[136,128]{1,0:T(8,128)S(1)}, u32[]{:S(2)}, u32[]{:S(2)}) %collective-permute-start) | collective-permute-done | bytes 69664 | tf_op jit(solution)/shard_map/ppermute | solution.py:277
  6.3 0.0 copy-start
  6.3 0.6 %copy-done = f32[136,128]{1,0:T(8,128)} copy-done((f32[136,128]{1,0:T(8,128)}, f32[136,128]{1,0:T(8,128)S(1)}, u32[]{:S(2)}) %copy-start) | copy-done | bytes 69656
  7.0 1.8 %chip_total.1.own_ref.refs_0_ = f32[136,128]{1,0:T(8,128)} custom-call(f32[136,128]{1,0:T(8,128)} %get-tuple-element.13.own_ref.refs_4_, f32[136,128]{1,0:T(8,128)} %copy-done), custom_call_target="tpu_custom_call" | custom-call | flops 2000000 | bytes 200000 | tf_op jit(solution)/shard_map/chip_total/pallas_call | solution.py:287
  8.7 2.6 %collective-permute-start.1 = (f32[136,128]{1,0:T(8,128)}, f32[136,128]{1,0:T(8,128)S(1)}, u32[]{:S(2)}, u32[]{:S(2)}) collective-permute-start(f32[136,128]{1,0:T(8,128)} %chip_total.1.own_ref.refs_0_), channel_id=1, source_target_pairs={{0,3},{1,2},{2,1},{3,0},{4,7},{5,6},{6,5},{7,4},{8,11},{9,10},{10,... | collective-permute-start | bytes 208904 | tf_op jit(solution)/shard_map/ppermute | solution.py:277
  11.3 1.5 %collective-permute-start.2 = (f32[136,128]{1,0:T(8,128)}, f32[136,128]{1,0:T(8,128)S(1)}, u32[]{:S(2)}, u32[]{:S(2)}) collective-permute-start(f32[136,128]{1,0:T(8,128)} %chip_total.1.own_ref.refs_0_), channel_id=1, source_target_pairs={{0,5},{1,4},{2,7},{3,6},{4,1},{5,0},{6,3},{7,2},{8,13},{9,12},{10,... | collective-permute-start | bytes 208904 | tf_op jit(solution)/shard_map/ppermute | solution.py:277
  12.9 0.0 collective-permute-start.3
  12.9 1.0 %collective-permute-done.1.refs_0_.refs_1_ = f32[136,128]{1,0:T(8,128)S(1)} collective-permute-done((f32[136,128]{1,0:T(8,128)}, f32[136,128]{1,0:T(8,128)S(1)}, u32[]{:S(2)}, u32[]{:S(2)}) %collective-permute-start.1) | collective-permute-done | bytes 69664 | tf_op jit(solution)/shard_map/ppermute | solution.py:277
  13.9 0.0 copy-start.1
  13.9 1.9 %collective-permute-done.2.refs_1_.refs_2_ = f32[136,128]{1,0:T(8,128)S(1)} collective-permute-done((f32[136,128]{1,0:T(8,128)}, f32[136,128]{1,0:T(8,128)S(1)}, u32[]{:S(2)}, u32[]{:S(2)}) %collective-permute-start.2) | collective-permute-done | bytes 69664 | tf_op jit(solution)/shard_map/ppermute | solution.py:277
  15.7 0.0 copy-start.2
  15.8 2.4 %collective-permute-done.3.refs_2_.refs_3_ = f32[136,128]{1,0:T(8,128)S(1)} collective-permute-done((f32[136,128]{1,0:T(8,128)}, f32[136,128]{1,0:T(8,128)S(1)}, u32[]{:S(2)}, u32[]{:S(2)}) %collective-permute-start.3) | collective-permute-done | bytes 69664 | tf_op jit(solution)/shard_map/ppermute | solution.py:277
  18.1 0.0 copy-start.3
  18.1 0.0 copy-done.1
  18.1 0.0 copy-done.2
  18.1 0.6 %copy-done.3 = f32[136,128]{1,0:T(8,128)} copy-done((f32[136,128]{1,0:T(8,128)}, f32[136,128]{1,0:T(8,128)S(1)}, u32[]{:S(2)}) %copy-start.3) | copy-done | bytes 69656
  18.7 2.2 %block_reach.1 = f32[8,128]{1,0:T(8,128)} custom-call(f32[8,128]{1,0:T(8,128)} %get-tuple-element.12.first_ref, f32[136,128]{1,0:T(8,128)} %chip_total.1.own_ref.refs_0_, f32[136,128]{1,0:T(8,128)} %copy-done.1, f32[136,128]{1,0:T(8,128)} %copy-done.2, f32[136,128]{1,0:T(8,128)} %copy-done.3), custom_call_target="tpu_custom_call" | custom-call | flops 2000000 | bytes 200000 | tf_op jit(solution)/shard_map/block_reach/pallas_call | solution.py:322
  20.9 2.4 %collective-permute-start.4 = (f32[8,128]{1,0:T(8,128)}, f32[8,128]{1,0:T(8,128)S(1)}, u32[]{:S(2)}, u32[]{:S(2)}) collective-permute-start(f32[8,128]{1,0:T(8,128)} %block_reach.1), channel_id=1, source_target_pairs={{0,9},{1,8},{2,11},{3,10},{4,13},{5,12},{6,15},{7,14},{8,1},{9,0},... | collective-permute-start | bytes 12296 | tf_op jit(solution)/shard_map/ppermute | solution.py:277
  23.3 1.8 %collective-permute-done.4 = f32[8,128]{1,0:T(8,128)S(1)} collective-permute-done((f32[8,128]{1,0:T(8,128)}, f32[8,128]{1,0:T(8,128)S(1)}, u32[]{:S(2)}, u32[]{:S(2)}) %collective-permute-start.4) | collective-permute-done | bytes 4128 | tf_op jit(solution)/shard_map/ppermute | solution.py:277
  25.1 0.0 copy-done.4
  25.1 0.6 %broadcast_select_fusion.entering_ref = f32[8,128]{1,0:T(8,128)} fusion(f32[8,128]{1,0:T(8,128)S(1)} %collective-permute-done.4, f32[8,128]{1,0:T(8,128)S(1)} %copy-done.4, pred[]{:T(512)S(6)} %ge.3), kind=kLoop, calls=%fused_computation | loop fusion | flops 1024 | bytes 12289 | tf_op jit(solution)/shard_map/jit(_where)/select_n | solution.py:334
  25.7 3.0 %finish.1 = f32[16,128]{1,0:T(8,128)} custom-call(f32[8,128]{1,0:T(8,128)} %broadcast_select_fusion.entering_ref, f32[16,128]{1,0:T(8,128)} %guess_ref.3, f32[64,256]{1,0:T(8,128)} %bitcast.5, f32[7,144,128]{2,1,0:T(8,128)} %get-tuple-element.14.tree_ref, f32[8,64,128]{2,1,0:T(8,128)} %get-tuple-element.15.kicks_ref, ...), custom_call_target="tpu_custom_call" | custom-call | flops 2000000 | bytes 200000 | tf_op jit(solution)/shard_map/finish/pallas_call | solution.py:351
  (1 shorter events, 0.0 us)
Async XLA Ops:
  4.7 1.6 %collective-permute-start = (f32[136,128]{1,0:T(8,128)}, f32[136,128]{1,0:T(8,128)S(1)}, u32[]{:S(2)}, u32[]{:S(2)}) collective-permute-start(f32[136,128]{1,0:T(8,128)} %get-tuple-element.13.own_ref.refs_4_), channel_id=1, source_target_pairs={{0,1},{1,0},{2,3},{3,2},{4,5},{5,4},{6,7},{7,6},{8,9},{9,8},{10,11... | collective-permute-start | bytes 208904 | tf_op jit(solution)/shard_map/ppermute | solution.py:277
  6.3 0.6 %copy-start = (f32[136,128]{1,0:T(8,128)}, f32[136,128]{1,0:T(8,128)S(1)}, u32[]{:S(2)}) copy-start(f32[136,128]{1,0:T(8,128)S(1)} %collective-permute-done.refs_0_.refs_5_) | copy-start | bytes 208900
  8.7 5.1 %collective-permute-start.1 = (f32[136,128]{1,0:T(8,128)}, f32[136,128]{1,0:T(8,128)S(1)}, u32[]{:S(2)}, u32[]{:S(2)}) collective-permute-start(f32[136,128]{1,0:T(8,128)} %chip_total.1.own_ref.refs_0_), channel_id=1, source_target_pairs={{0,3},{1,2},{2,1},{3,0},{4,7},{5,6},{6,5},{7,4},{8,11},{9,10},{10,... | collective-permute-start | bytes 208904 | tf_op jit(solution)/shard_map/ppermute | solution.py:277
  11.3 4.4 %collective-permute-start.2 = (f32[136,128]{1,0:T(8,128)}, f32[136,128]{1,0:T(8,128)S(1)}, u32[]{:S(2)}, u32[]{:S(2)}) collective-permute-start(f32[136,128]{1,0:T(8,128)} %chip_total.1.own_ref.refs_0_), channel_id=1, source_target_pairs={{0,5},{1,4},{2,7},{3,6},{4,1},{5,0},{6,3},{7,2},{8,13},{9,12},{10,... | collective-permute-start | bytes 208904 | tf_op jit(solution)/shard_map/ppermute | solution.py:277
  12.9 5.3 %collective-permute-start.3 = (f32[136,128]{1,0:T(8,128)}, f32[136,128]{1,0:T(8,128)S(1)}, u32[]{:S(2)}, u32[]{:S(2)}) collective-permute-start(f32[136,128]{1,0:T(8,128)} %chip_total.1.own_ref.refs_0_), channel_id=1, source_target_pairs={{0,7},{1,6},{2,5},{3,4},{4,3},{5,2},{6,1},{7,0},{8,15},{9,14},{10,... | collective-permute-start | bytes 208904 | tf_op jit(solution)/shard_map/ppermute | solution.py:277
  13.9 4.2 %copy-start.1 = (f32[136,128]{1,0:T(8,128)}, f32[136,128]{1,0:T(8,128)S(1)}, u32[]{:S(2)}) copy-start(f32[136,128]{1,0:T(8,128)S(1)} %collective-permute-done.1.refs_0_.refs_1_) | copy-start | bytes 208900
  15.7 2.4 %copy-start.2 = (f32[136,128]{1,0:T(8,128)}, f32[136,128]{1,0:T(8,128)S(1)}, u32[]{:S(2)}) copy-start(f32[136,128]{1,0:T(8,128)S(1)} %collective-permute-done.2.refs_1_.refs_2_) | copy-start | bytes 208900
  18.1 0.6 %copy-start.3 = (f32[136,128]{1,0:T(8,128)}, f32[136,128]{1,0:T(8,128)S(1)}, u32[]{:S(2)}) copy-start(f32[136,128]{1,0:T(8,128)S(1)} %collective-permute-done.3.refs_2_.refs_3_) | copy-start | bytes 208900
  20.9 4.1 %collective-permute-start.4 = (f32[8,128]{1,0:T(8,128)}, f32[8,128]{1,0:T(8,128)S(1)}, u32[]{:S(2)}, u32[]{:S(2)}) collective-permute-start(f32[8,128]{1,0:T(8,128)} %block_reach.1), channel_id=1, source_target_pairs={{0,9},{1,8},{2,11},{3,10},{4,13},{5,12},{6,15},{7,14},{8,1},{9,0},... | collective-permute-start | bytes 12296 | tf_op jit(solution)/shard_map/ppermute | solution.py:277
  23.3 1.8 %copy-start.4 = (f32[8,128]{1,0:T(8,128)S(1)}, f32[8,128]{1,0:T(8,128)}, u32[]{:S(2)}) copy-start(f32[8,128]{1,0:T(8,128)} %get-tuple-element.12.first_ref) | copy-start | bytes 12292

commit v2 on v1

--- a/solution.py
+++ b/solution.py
@@ -31,8 +31,19 @@
     return jnp.concatenate([product[:state], product[state:] + late[state:]], axis=0)
 
 
-def local_kernel(guess_ref, start_ref, weight_ref, bias_ref, amp_ref,
-                 total_ref, first_ref, tree_ref, kicks_ref, kick_first_ref, shifts_ref, curve_ref):
+def local_kernel(guess_in, start_in, weight_in, bias_in, amp_in,
+                 total_ref, first_ref, tree_ref, kicks_ref, kick_first_ref, shifts_ref, curve_ref, guess_ref, weight_ref,
+                 start_ref, bias_ref, amp_ref, arrived):
+    copies = [
+        pltpu.make_async_copy(source, target, arrived.at[index])
+        for index, (source, target) in enumerate((
+            (weight_in, weight_ref), (guess_in, guess_ref), (start_in, start_ref),
+            (bias_in, bias_ref), (amp_in, amp_ref)))
+    ]
+    for copy in copies:
+        copy.start()
+    for copy in copies:
+        copy.wait()
     rows, state = guess_ref.shape
     width = state // 2
     h = step_size
@@ -227,11 +238,13 @@
     out_ref[...] = jnp.where(row_id == 0, jnp.broadcast_to(state[0:1], (rows, size)), result)
 
 
-def call(kernel, out_shape, scratch=(), flops=2_000_000, name=None):
+def call(kernel, out_shape, scratch=(), flops=2_000_000, name=None, **specs):
     return pl.pallas_call(
         kernel,
+        **specs,
         out_shape=out_shape,
         scratch_shapes=scratch,
+        compiler_params=pltpu.CompilerParams(vmem_limit_bytes=8 << 20),
         cost_estimate=pl.CostEstimate(flops=flops, bytes_accessed=200_000, transcendentals=0),
         name=name,
     )
@@ -266,12 +279,15 @@
         packed = f32((size + 8, size))
         weight_t = layer_weight.T
         nodes = rows // 2 - 1
-        total, first, tree, kicks, kick_first, shifts, curve = call(
+        total, first, tree, kicks, kick_first, shifts, curve, guess, weight_t = call(
             local_kernel,
             [packed, f32((8, size)), f32((nodes, size + PAD, size)), f32((rows // 2, width, size)),
-             f32((width, size)), f32((rows, size)), f32((rows, hidden))],
-            name="local_maps", flops=100_000_000,
-        )(guess, start[None, :], weight_t, layer_bias[None, :], amplitude[None, :])
+             f32((width, size)), f32((rows, size)), f32((rows, hidden)), f32((rows, size)), f32((width, hidden))],
+            [pltpu.VMEM((1, size), jnp.float32), pltpu.VMEM((1, hidden), jnp.float32), pltpu.VMEM((1, hidden), jnp.float32),
+             pltpu.SemaphoreType.DMA((5,))],
+            name="local_maps", flops=100_000_000, in_specs=[pl.BlockSpec(memory_space=pltpu.HBM)] * 5,
+        )(*(pltpu.with_memory_space_constraint(value, pltpu.HBM) for value in (
+            guess, start[None, :], weight_t, layer_bias[None, :], amplitude[None, :])))
 
         def exchange(value, pairs):
             return lax.ppermute(value, axes, pairs)

time: 28.9 us -> 21.4 us (0.74)
  Pallas kernels: 11.7 us -> 6.59 us
  local copies, waits for them, and re-layouts: 1.25 us -> 0 us
  waiting for transfers between devices: 8.15 us -> 7.54 us
  other arithmetic: 0.59 us -> 0.01 us
    pallas_call x1, Pallas kernels: 2.18 us -> 0.57 us  [shards(): call(functools.partial(reach_kernel, group_source, group_place, group), f...]
    pallas_call x1, Pallas kernels: 1.77 us -> 0.22 us  [shards(): call(functools.partial(total_kernel, inner_source, inner_place, inners),...]
    pallas_call x1, Pallas kernels: 3.01 us -> 1.71 us  [shards(): call(functools.partial(finish_kernel, groups, rows), f32((rows, size)), s...]
    unnamed x10 -> x0, local copies, waits for them, and re-layouts: 1.25 us -> none
    pallas_call x1, Pallas kernels: 4.73 us -> 4.09 us  [shards(): call(local_kernel, [packed, f32((8, size)), f32((nodes, size + PAD, size)...]
    ppermute x5, waiting for transfers between devices: 8.15 us -> 7.54 us  [exchange(): return lax.ppermute(value, axes, pairs)]
    select_n x1, other arithmetic: 0.59 us -> 0.01 us  [shards(): entering = jnp.where(block >= top, arrived, first)]
where the time goes in v2:
time: 21.4 us; the launch traced here: 21.3 us
  waiting for transfers between devices  7.54 us (35%)
  starting transfers between devices  7.12 us (33%)
  Pallas kernels  6.59 us (31%)
    ppermute x5, waiting for transfers between devices, exchange(): return lax.ppermute(value, axes, pairs)  7.54 us
    ppermute x5, starting transfers between devices, exchange(): return lax.ppermute(value, axes, pairs)  7.12 us
    pallas_call x1, Pallas kernels, shards(): call(local_kernel, [packed, f32((8, size)), f32((nodes, size + PAD, size)...  4.09 us
    pallas_call x1, Pallas kernels, shards(): call(functools.partial(finish_kernel, groups, rows), f32((rows, size)), s...  1.71 us
    pallas_call x1, Pallas kernels, shards(): call(functools.partial(reach_kernel, group_source, group_place, group), f...  0.57 us
  transfers between devices with their start and end apart: 5, of which 5 were waited for; matrix products, arithmetic and copies ran while one was open for 0% of the time, Pallas kernels for 0%

profile of v2, /device:TPU:0, one launch (start us, length us, event | category | flops | bytes accessed | tf_op | source)
XLA Modules:
  0.0 21.3 jit_solution(412882638687857545)
XLA Ops:
  0.0 4.1 %local_maps.1 = (f32[136,128]{1,0:T(8,128)S(1)}, f32[8,128]{1,0:T(8,128)S(1)}, f32[7,144,128]{2,1,0:T(8,128)S(1)}, f32[8,64,128]{2,1,0:T(8,128)S(1)}, f32[64,128...) custom-call(f32[16,128]{1,0:T(8,128)} %guess_in.1, ...), custom_call_target="tpu_custom_call" | custom-call | flops 100000000 | bytes 200000 | tf_op jit(solution)/shard_map/local_maps/pallas_call | solution.py:282
  4.1 0.6 %collective-permute-start = (f32[136,128]{1,0:T(8,128)S(1)}, f32[136,128]{1,0:T(8,128)S(1)}, u32[]{:S(2)}, u32[]{:S(2)}) collective-permute-start(f32[136,128]{1,0:T(8,128)S(1)} %get-tuple-element.15.own_ref.refs_4_), channel_id=1, source_target_pairs={{0,1},{1,0},{2,3},{3,2},{4,5},{5,4},{6,7},{7,6},{8,9},{9,8},{10,11... | collective-permute-start | bytes 208904 | tf_op jit(solution)/shard_map/ppermute | solution.py:293
  4.7 0.9 %collective-permute-done.refs_0_.refs_5_ = f32[136,128]{1,0:T(8,128)S(1)} collective-permute-done((f32[136,128]{1,0:T(8,128)S(1)}, f32[136,128]{1,0:T(8,128)S(1)}, u32[]{:S(2)}, u32[]{:S(2)}) %collective-permute-start) | collective-permute-done | bytes 69664 | tf_op jit(solution)/shard_map/ppermute | solution.py:293
  5.6 0.2 %chip_total.1.own_ref.refs_0_ = f32[136,128]{1,0:T(8,128)S(1)} custom-call(f32[136,128]{1,0:T(8,128)S(1)} %get-tuple-element.15.own_ref.refs_4_, f32[136,128]{1,0:T(8,128)S(1)} %collective-permute-done.refs_0_.refs_5_), custom_call_target="tpu_custom_call" | custom-call | flops 2000000 | bytes 200000 | tf_op jit(solution)/shard_map/chip_total/pallas_call | solution.py:303
  5.8 2.7 %collective-permute-start.1 = (f32[136,128]{1,0:T(8,128)S(1)}, f32[136,128]{1,0:T(8,128)S(1)}, u32[]{:S(2)}, u32[]{:S(2)}) collective-permute-start(f32[136,128]{1,0:T(8,128)S(1)} %chip_total.1.own_ref.refs_0_), channel_id=1, source_target_pairs={{0,3},{1,2},{2,1},{3,0},{4,7},{5,6},{6,5},{7,4},{8,11},{9,10},{10,... | collective-permute-start | bytes 208904 | tf_op jit(solution)/shard_map/ppermute | solution.py:293
  8.4 1.5 %collective-permute-start.2 = (f32[136,128]{1,0:T(8,128)S(1)}, f32[136,128]{1,0:T(8,128)S(1)}, u32[]{:S(2)}, u32[]{:S(2)}) collective-permute-start(f32[136,128]{1,0:T(8,128)S(1)} %chip_total.1.own_ref.refs_0_), channel_id=1, source_target_pairs={{0,5},{1,4},{2,7},{3,6},{4,1},{5,0},{6,3},{7,2},{8,13},{9,12},{10,... | collective-permute-start | bytes 208904 | tf_op jit(solution)/shard_map/ppermute | solution.py:293
  10.0 0.0 collective-permute-start.3
  10.0 0.7 %collective-permute-done.1.refs_0_.refs_1_ = f32[136,128]{1,0:T(8,128)S(1)} collective-permute-done((f32[136,128]{1,0:T(8,128)S(1)}, f32[136,128]{1,0:T(8,128)S(1)}, u32[]{:S(2)}, u32[]{:S(2)}) %collective-permute-start.1) | collective-permute-done | bytes 69664 | tf_op jit(solution)/shard_map/ppermute | solution.py:293
  10.7 1.9 %collective-permute-done.2.refs_1_.refs_2_ = f32[136,128]{1,0:T(8,128)S(1)} collective-permute-done((f32[136,128]{1,0:T(8,128)S(1)}, f32[136,128]{1,0:T(8,128)S(1)}, u32[]{:S(2)}, u32[]{:S(2)}) %collective-permute-start.2) | collective-permute-done | bytes 69664 | tf_op jit(solution)/shard_map/ppermute | solution.py:293
  12.6 2.5 %collective-permute-done.3.refs_2_.refs_3_ = f32[136,128]{1,0:T(8,128)S(1)} collective-permute-done((f32[136,128]{1,0:T(8,128)S(1)}, f32[136,128]{1,0:T(8,128)S(1)}, u32[]{:S(2)}, u32[]{:S(2)}) %collective-permute-start.3) | collective-permute-done | bytes 69664 | tf_op jit(solution)/shard_map/ppermute | solution.py:293
  15.0 0.6 %block_reach.1 = f32[8,128]{1,0:T(8,128)S(1)} custom-call(f32[8,128]{1,0:T(8,128)S(1)} %get-tuple-element.14.first_ref, f32[136,128]{1,0:T(8,128)S(1)} %chip_total.1.own_ref.refs_0_, f32[136,128]{1,0:T(8,128)S(1)} %collective-permute-done.1.refs_0_.refs_1_, f32[136,128]{1,0:T(8,128)S(1)} %collective-permute-done.2.refs_1_.refs_2_, ...), custom_call_target="tpu_custom_call" | custom-call | flops 2000000 | bytes 200000 | tf_op jit(solution)/shard_map/block_reach/pallas_call | solution.py:338
  15.6 2.4 %collective-permute-start.4 = (f32[8,128]{1,0:T(8,128)S(1)}, f32[8,128]{1,0:T(8,128)S(1)}, u32[]{:S(2)}, u32[]{:S(2)}) collective-permute-start(f32[8,128]{1,0:T(8,128)S(1)} %block_reach.1), channel_id=1, source_target_pairs={{0,9},{1,8},{2,11},{3,10},{4,13},{5,12},{6,15},{7,14},{8,1},{9,0},... | collective-permute-start | bytes 12296 | tf_op jit(solution)/shard_map/ppermute | solution.py:293
  18.0 1.6 %collective-permute-done.4 = f32[8,128]{1,0:T(8,128)S(1)} collective-permute-done((f32[8,128]{1,0:T(8,128)S(1)}, f32[8,128]{1,0:T(8,128)S(1)}, u32[]{:S(2)}, u32[]{:S(2)}) %collective-permute-start.4) | collective-permute-done | bytes 4128 | tf_op jit(solution)/shard_map/ppermute | solution.py:293
  19.6 1.7 %finish.1 = f32[16,128]{1,0:T(8,128)} custom-call(f32[8,128]{1,0:T(8,128)S(1)} %broadcast_select_fusion.entering_ref, f32[16,128]{1,0:T(8,128)S(1)} %get-tuple-element.16.guess_ref, f32[64,256]{1,0:T(8,128)S(1)} %get-tuple-element.17.weight_ref, f32[7,144,128]{2,1,0:T(8,128)S(1)} %get-tuple-element.18.tree_ref, ...), custom_call_target="tpu_custom_call" | custom-call | flops 2000000 | bytes 200000 | tf_op jit(solution)/shard_map/finish/pallas_call | solution.py:367
  (1 shorter events, 0.0 us)
Async XLA Ops:
  4.1 1.5 %collective-permute-start = (f32[136,128]{1,0:T(8,128)S(1)}, f32[136,128]{1,0:T(8,128)S(1)}, u32[]{:S(2)}, u32[]{:S(2)}) collective-permute-start(f32[136,128]{1,0:T(8,128)S(1)} %get-tuple-element.15.own_ref.refs_4_), channel_id=1, source_target_pairs={{0,1},{1,0},{2,3},{3,2},{4,5},{5,4},{6,7},{7,6},{8,9},{9,8},{10,11... | collective-permute-start | bytes 208904 | tf_op jit(solution)/shard_map/ppermute | solution.py:293
  5.8 4.9 %collective-permute-start.1 = (f32[136,128]{1,0:T(8,128)S(1)}, f32[136,128]{1,0:T(8,128)S(1)}, u32[]{:S(2)}, u32[]{:S(2)}) collective-permute-start(f32[136,128]{1,0:T(8,128)S(1)} %chip_total.1.own_ref.refs_0_), channel_id=1, source_target_pairs={{0,3},{1,2},{2,1},{3,0},{4,7},{5,6},{6,5},{7,4},{8,11},{9,10},{10,... | collective-permute-start | bytes 208904 | tf_op jit(solution)/shard_map/ppermute | solution.py:293
  8.4 4.1 %collective-permute-start.2 = (f32[136,128]{1,0:T(8,128)S(1)}, f32[136,128]{1,0:T(8,128)S(1)}, u32[]{:S(2)}, u32[]{:S(2)}) collective-permute-start(f32[136,128]{1,0:T(8,128)S(1)} %chip_total.1.own_ref.refs_0_), channel_id=1, source_target_pairs={{0,5},{1,4},{2,7},{3,6},{4,1},{5,0},{6,3},{7,2},{8,13},{9,12},{10,... | collective-permute-start | bytes 208904 | tf_op jit(solution)/shard_map/ppermute | solution.py:293
  10.0 5.0 %collective-permute-start.3 = (f32[136,128]{1,0:T(8,128)S(1)}, f32[136,128]{1,0:T(8,128)S(1)}, u32[]{:S(2)}, u32[]{:S(2)}) collective-permute-start(f32[136,128]{1,0:T(8,128)S(1)} %chip_total.1.own_ref.refs_0_), channel_id=1, source_target_pairs={{0,7},{1,6},{2,5},{3,4},{4,3},{5,2},{6,1},{7,0},{8,15},{9,14},{10,... | collective-permute-start | bytes 208904 | tf_op jit(solution)/shard_map/ppermute | solution.py:293
  15.6 4.0 %collective-permute-start.4 = (f32[8,128]{1,0:T(8,128)S(1)}, f32[8,128]{1,0:T(8,128)S(1)}, u32[]{:S(2)}, u32[]{:S(2)}) collective-permute-start(f32[8,128]{1,0:T(8,128)S(1)} %block_reach.1), channel_id=1, source_target_pairs={{0,9},{1,8},{2,11},{3,10},{4,13},{5,12},{6,15},{7,14},{8,1},{9,0},... | collective-permute-start | bytes 12296 | tf_op jit(solution)/shard_map/ppermute | solution.py:293

commit v3 on v2

--- a/solution.py
+++ b/solution.py
@@ -25,15 +25,22 @@
     return one(left_high, right_high) + (one(left_high, right_low) + one(left_low, right_high))
 
 
+def dot3w(left, right):
+    (left_high, left_low), (right_high, right_low) = left, right
+    size = right_high.shape[1]
+    both = jnp.dot(left_high, jnp.concatenate([right_high, right_low], axis=1), preferred_element_type=jnp.float32)
+    return both[:, :size] + (both[:, size:] + jnp.dot(left_low, right_high, preferred_element_type=jnp.float32))
+
+
 def join(early, late):
     state = late.shape[1]
-    product = dot3(split(early), split(late[:state]))
+    product = dot3w(split(early), split(late[:state]))
     return jnp.concatenate([product[:state], product[state:] + late[state:]], axis=0)
 
 
 def local_kernel(guess_in, start_in, weight_in, bias_in, amp_in,
                  total_ref, first_ref, tree_ref, kicks_ref, kick_first_ref, shifts_ref, curve_ref, guess_ref, weight_ref,
-                 start_ref, bias_ref, amp_ref, arrived):
+                 start_ref, bias_ref, amp_ref, high_ref, low_ref, arrived):
     copies = [
         pltpu.make_async_copy(source, target, arrived.at[index])
         for index, (source, target) in enumerate((
@@ -90,13 +97,20 @@
     unit_low = jnp.where(lane == line + width, 1.0, 0.0)
     between = (curve_one[:rows] + curve_next) * (0.5 * h)
 
-    def kick(weights_row, count):
-        scaled = weight * weights_row
-        return dot3(split(scaled), double2, NT) + (0.5 * h * curvature * count) * unit2
-
-    kick_first = kick(curve_zero[0:1] * (0.5 * h), 1)
+    rows_of_kick = [curve_zero[0:1] * (0.5 * h)] + [between[j:j + 1] for j in range(rows)]
+    for j, weights_row in enumerate(rows_of_kick):
+        scaled_high, scaled_low = split(weight * weights_row)
+        high_ref[j * width:(j + 1) * width] = scaled_high
+        low_ref[j * width:(j + 1) * width] = scaled_low
+    product = lax.dot_general(high_ref[...], jnp.concatenate(double2, axis=0), NT, preferred_element_type=jnp.float32)
+    small = lax.dot_general(low_ref[...], double2[0], NT, preferred_element_type=jnp.float32)
+    product = product[:, :state] + (product[:, state:] + small)
+    kicks = [
+        product[j * width:(j + 1) * width] + (0.5 * h * curvature * (1 if j in (0, rows) else 2)) * unit2
+        for j in range(rows + 1)
+    ]
+    kick_first, kicks = kicks[0], kicks[1:]
     kick_first_ref[...] = kick_first
-    kicks = [kick(between[j:j + 1], 2 if j < rows - 1 else 1) for j in range(rows)]
     for j in range(0, rows, 2):
         kicks_ref[j // 2] = kicks[j]
 
@@ -173,69 +187,95 @@
     out_ref[...] = state
 
 
-def finish_kernel(groups, rows, entering_ref, guess_ref, weight_ref, tree_ref, kicks_ref, kick_first_ref,
-                  shifts_ref, curve_ref, *refs):
-    size = guess_ref.shape[1]
+def prefix_kernel(tree_ref, kicks_ref, kick_first_ref, shifts_ref, curve_ref, guess_ref, weight_ref,
+                  maps_ref, offsets_ref, high_ref, low_ref):
+    rows, size = guess_ref.shape
     width = size // 2
     h = step_size
-    out_ref = refs[-1 - len(groups)]
+    weight = weight_ref[...]
+    double2 = split(jnp.concatenate([weight, weight], axis=0))
+    for j in range(1, rows):
+        scaled_high, scaled_low = split(weight * (curve_ref[j:j + 1] * (0.5 * h)))
+        high_ref[(j - 1) * width:j * width] = scaled_high
+        low_ref[(j - 1) * width:j * width] = scaled_low
+    product = lax.dot_general(high_ref[...], jnp.concatenate(double2, axis=0), NT, preferred_element_type=jnp.float32)
+    small = lax.dot_general(low_ref[...], double2[0], NT, preferred_element_type=jnp.float32)
+    product = product[:, :size] + (product[:, size:] + small)
+    line = lax.broadcasted_iota(jnp.int32, (width, size), 0)
+    lane = lax.broadcasted_iota(jnp.int32, (width, size), 1)
+    unit2 = jnp.where((lane == line) | (lane == line + width), 0.5 * h * curvature, 0.0)
+    whole_line = lax.broadcasted_iota(jnp.int32, (size + PAD, size), 0)
+    whole_lane = lax.broadcasted_iota(jnp.int32, (size + PAD, size), 1)
+    left = whole_lane < width
+    unit = jnp.where(whole_line == whole_lane, 1.0, 0.0)
+
+    def kick(item, matrix):
+        return item - jnp.where(left, 0.0, dot3w(split(item[:, :width]), split(matrix)))
+
+    def drift(item):
+        other = jnp.concatenate([item[:, width:], item[:, :width]], axis=1)
+        return item + jnp.where(left, h * other, 0.0)
+
+    count = rows // 2
+    starts, sizes, n = [0], [], count
+    while n > 1:
+        sizes.append(n // 2)
+        starts.append(starts[-1] + n // 2)
+        n //= 2
+    kicked = {0: kick(unit, kick_first_ref[...])}
+    for k in range(1, count):
+        low = k & -k
+        node = tree_ref[starts[low.bit_length() - 1] + (k - low) // low // 2]
+        kicked[2 * k] = node if k == low else join(kicked[2 * (k - low)], node)
+    maps_ref[0] = unit[:size]
+    offsets_ref[0:1] = guess_ref[0:1]
+    for k in range(count):
+        after = kick(drift(kicked[2 * k]), kicks_ref[k])
+        tail = after[size:] + shifts_ref[2 * k:2 * k + 1]
+        kicked[2 * k + 1] = jnp.concatenate([after[:size], tail], axis=0)
+    for t in range(1, rows):
+        item = kick(kicked[t], -(product[(t - 1) * width:t * width] + unit2))
+        maps_ref[t] = item[:size]
+        offsets_ref[t:t + 1] = item[size:size + 1] + guess_ref[t:t + 1]
+
+
+def ahead_kernel(groups, guess_ref, *refs):
+    size = guess_ref.shape[1]
+    out_ref, shift_ref, origin_ref = refs[-3 - len(groups):len(refs) - len(groups)]
     stacks = refs[len(refs) - len(groups):]
-    state = entering_ref[...]
+    line = lax.broadcasted_iota(jnp.int32, (size + 8, size), 0)
+    lane = lax.broadcasted_iota(jnp.int32, (size + 8, size), 1)
+    total = jnp.where(line == lane, 1.0, 0.0)
+    empty = True
     used = 0
     for (source, axis_place, count), stack_ref in zip(groups, stacks):
         own_ref, others = refs[used], refs[used + 1:used + count]
         used += count
         place = axis_place()
         ordered(own_ref, others, stack_ref, place, source)
-        state = lax.fori_loop(0, place, lambda i, s, stack_ref=stack_ref: apply(s, stack_ref[i]), state)
-    guess = guess_ref[...]
-    delta = state - guess[0:1]
-
-    def go(vector, item):
-        return dot3(split(vector), split(item[:size])) + item[size:size + 8]
-
-    count = rows // 2
-    sizes = []
-    n = count
-    while n > 1:
-        sizes.append((n + 1) // 2)
-        n //= 2
-    starts = [sum(sizes[:i]) for i in range(len(sizes))]
-    offsets = {0: delta}
-    span = count
-    for lev in reversed(range(len(sizes))):
-        span //= 2
-        for i in range(sizes[lev]):
-            offsets[(2 * i + 1) * span] = go(offsets[2 * i * span], tree_ref[starts[lev] + i])
-
-    left = lax.broadcasted_iota(jnp.int32, (8, size), 1) < width
-
-    def kick(vector, matrix):
-        moved = dot3(split(vector[:, :width]), split(matrix))
-        return vector - jnp.where(left, 0.0, moved)
-
-    def drift(vector):
-        other = jnp.concatenate([vector[:, width:], vector[:, :width]], axis=1)
-        return vector + jnp.where(left, h * other, 0.0)
-
-    pieces = []
-    for i in range(count):
-        begin = offsets[i]
-        if i > 0:
-            pieces.append(begin[0:1])
+
+        def body(i, carry, stack_ref=stack_ref):
+            return compose(carry, stack_ref[i])
+
+        if empty is True:
+            total = lax.fori_loop(1, place, body, jnp.where(place > 0, stack_ref[0], total))
+            empty = place == 0
         else:
-            pieces.append(jnp.zeros((1, size), jnp.float32))
-            begin = kick(begin, kick_first_ref[...])
-        after = kick(drift(begin), kicks_ref[i]) + shifts_ref[2 * i:2 * i + 1]
-        pieces.append(after[0:1])
-    kicked = jnp.concatenate(pieces, axis=0)
-    weight2 = split(weight_ref[...])
-    pushed = kicked[:, :width]
-    inner = dot3(split(pushed), weight2) * curve_ref[...]
-    back = 0.5 * h * (dot3(split(inner), weight2, NT) + curvature * pushed)
-    result = kicked + jnp.concatenate([jnp.zeros_like(back), back], axis=1) + guess
-    row_id = lax.broadcasted_iota(jnp.int32, (rows, size), 0)
-    out_ref[...] = jnp.where(row_id == 0, jnp.broadcast_to(state[0:1], (rows, size)), result)
+            first = jnp.where(empty, stack_ref[0], compose(total, stack_ref[0]))
+            total = lax.fori_loop(1, place, body, jnp.where(place > 0, first, total))
+            empty = empty & (place == 0)
+    out_ref[...] = total[:size].T
+    shift = total[size:size + 1] - guess_ref[0:1]
+    shift_ref[...] = jnp.broadcast_to(shift, (size, size)).T
+    origin_ref[...] = jnp.broadcast_to(total[size + 1:size + 2], (8, size))
+
+
+def finish_kernel(later_block, arrived_ref, first_ref, ahead_ref, shift_ref, origin_ref, maps_ref, offsets_ref, out_ref):
+    rows, size = offsets_ref.shape
+    state = jnp.where(later_block(), arrived_ref[0:1], first_ref[0:1]) - origin_ref[0:1]
+    delta = jnp.sum(ahead_ref[...] * state, axis=1, keepdims=True) + shift_ref[...]
+    pieces = [jnp.sum(maps_ref[t] * delta, axis=0, keepdims=True) for t in range(rows)]
+    out_ref[...] = jnp.concatenate(pieces, axis=0) + offsets_ref[...]
 
 
 def call(kernel, out_shape, scratch=(), flops=2_000_000, name=None, **specs):
@@ -284,6 +324,7 @@
             [packed, f32((8, size)), f32((nodes, size + PAD, size)), f32((rows // 2, width, size)),
              f32((width, size)), f32((rows, size)), f32((rows, hidden)), f32((rows, size)), f32((width, hidden))],
             [pltpu.VMEM((1, size), jnp.float32), pltpu.VMEM((1, hidden), jnp.float32), pltpu.VMEM((1, hidden), jnp.float32),
+             pltpu.VMEM(((rows + 1) * width, hidden), jnp.bfloat16), pltpu.VMEM(((rows + 1) * width, hidden), jnp.bfloat16),
              pltpu.SemaphoreType.DMA((5,))],
             name="local_maps", flops=100_000_000, in_specs=[pl.BlockSpec(memory_space=pltpu.HBM)] * 5,
         )(*(pltpu.with_memory_space_constraint(value, pltpu.HBM) for value in (
@@ -312,6 +353,11 @@
 
         entering = first
         ahead = []
+        held = lax.optimization_barrier((tree, kicks, chip))[:2]
+        local, offsets = call(
+            prefix_kernel, [f32((rows, size, size)), f32((rows, size))],
+            [pltpu.VMEM(((rows - 1) * width, hidden), jnp.bfloat16)] * 2, name="local_prefix", flops=20_000_000_000,
+        )(*held, kick_first, shifts, curve, guess, weight_t)
         if blocks > 1:
             block = lax.axis_index("tm") // low
             top = 1
@@ -347,7 +393,10 @@
                 pairs = [(flat(b, g, i), flat((b + top) % blocks, g, (i + 1) % inners))
                          for b in range(blocks) for g in range(group) for i in range(inners)]
             arrived = exchange(reach, pairs)
-            entering = jnp.where(block >= top, arrived, first)
+            if blocks == 2:
+                entering = arrived
+            else:
+                entering = jnp.where(block >= top, arrived, first)
             for upper, value in reversed(ahead):
                 moved = call(lambda f_ref, m_ref, o_ref: o_ref.__setitem__(..., apply(f_ref[...], m_ref[...])),
                              f32((8, size)), name="span_step")(entering, value)
@@ -364,8 +413,15 @@
             groups.append((inner_source, inner_place, inners))
             maps += inner_maps
             scratch.append(pltpu.VMEM((inners,) + packed.shape, jnp.float32))
-        return call(functools.partial(finish_kernel, groups, rows), f32((rows, size)), scratch, name="finish")(
-            entering, guess, weight_t, tree, kicks, kick_first, shifts, curve, *maps)
+        scale, shift, base = call(
+            functools.partial(ahead_kernel, groups), [f32((size, size)), f32((size, size)), f32((8, size))], scratch,
+            name="block_prefix", flops=2_000_000_000)(guess, *maps)
+
+        def later_block():
+            return lax.axis_index("tm") >= low if blocks == 2 else blocks > 2
+
+        return call(functools.partial(finish_kernel, later_block), f32((rows, size)), name="finish")(
+            entering, first, scale, shift, base, local, offsets)
 
     placed = (P(("parts",) + axes, None), P("parts"), P(), P(), P())
     return jax.shard_map(

time: 21.4 us -> 18.7 us (0.87)
  waiting for transfers between devices: 7.54 us -> 4.45 us
  Pallas kernels: 6.59 us -> 6.82 us
    ppermute x5, waiting for transfers between devices: 7.54 us -> 4.45 us  [exchange(): return lax.ppermute(value, axes, pairs)]
    pallas_call x1 -> x3, Pallas kernels: 1.71 us -> 2.76 us  [the longest x1 1.63 us: shards(): call(prefix_kernel, [f32((rows, size, size)), f32((rows, size))], [pltpu....]
    pallas_call x1, Pallas kernels: 4.09 us -> 3.27 us  [shards(): call(local_kernel, [packed, f32((8, size)), f32((nodes, size + PAD, size)...]
  transfers between devices with their start and end apart: 5 -> 5, of which waited for: 5 -> 5; matrix products, arithmetic and copies ran while one was open for 0% -> 0% of each run, Pallas kernels for 0% -> 11%
where the time goes in v3:
time: 18.7 us; the launch traced here: 18.5 us
  starting transfers between devices  7.19 us (38%)
  Pallas kernels  6.82 us (36%)
  waiting for transfers between devices  4.45 us (24%)
    ppermute x5, starting transfers between devices, exchange(): return lax.ppermute(value, axes, pairs)  7.19 us
    ppermute x5, waiting for transfers between devices, exchange(): return lax.ppermute(value, axes, pairs)  4.45 us
    pallas_call x1, Pallas kernels, shards(): call(local_kernel, [packed, f32((8, size)), f32((nodes, size + PAD, size)...  3.27 us
    pallas_call x1, Pallas kernels, shards(): call(prefix_kernel, [f32((rows, size, size)), f32((rows, size))], [pltpu....  1.63 us
    pallas_call x1, Pallas kernels, shards(): call(functools.partial(finish_kernel, later_block), f32((rows, size)), na...  0.78 us
    pallas_call x1, Pallas kernels, shards(): call(functools.partial(reach_kernel, group_source, group_place, group), f...  0.58 us
  transfers between devices with their start and end apart: 5, of which 5 were waited for; matrix products, arithmetic and copies ran while one was open for 0% of the time, Pallas kernels for 11%

profile of v3, /device:TPU:0, one launch (start us, length us, event | category | flops | bytes accessed | tf_op | source)
XLA Modules:
  0.0 18.5 jit_solution(7821701939564193517)
XLA Ops:
  0.0 3.3 %local_maps.1 = (f32[136,128]{1,0:T(8,128)S(1)}, f32[8,128]{1,0:T(8,128)S(1)}, f32[7,144,128]{2,1,0:T(8,128)S(1)}, f32[8,64,128]{2,1,0:T(8,128)S(1)}, f32[64,128...) custom-call(f32[16,128]{1,0:T(8,128)} %guess_in.1, ...), custom_call_target="tpu_custom_call" | custom-call | flops 100000000 | bytes 200000 | tf_op jit(solution)/shard_map/local_maps/pallas_call | solution.py:322
  3.3 0.6 %collective-permute-start = (f32[136,128]{1,0:T(8,128)S(1)}, f32[136,128]{1,0:T(8,128)S(1)}, u32[]{:S(2)}, u32[]{:S(2)}) collective-permute-start(f32[136,128]{1,0:T(8,128)S(1)} %get-tuple-element.22.own_ref.refs_4_), channel_id=1, source_target_pairs={{0,1},{1,0},{2,3},{3,2},{4,5},{5,4},{6,7},{7,6},{8,9},{9,8},{10,11... | collective-permute-start | bytes 208904 | tf_op jit(solution)/shard_map/ppermute | solution.py:334
  3.8 0.9 %collective-permute-done.refs_0_.refs_5_ = f32[136,128]{1,0:T(8,128)S(1)} collective-permute-done((f32[136,128]{1,0:T(8,128)S(1)}, f32[136,128]{1,0:T(8,128)S(1)}, u32[]{:S(2)}, u32[]{:S(2)}) %collective-permute-start) | collective-permute-done | bytes 69664 | tf_op jit(solution)/shard_map/ppermute | solution.py:334
  4.7 0.2 %chip_total.1.own_ref.refs_0_ = f32[136,128]{1,0:T(8,128)S(1)} custom-call(f32[136,128]{1,0:T(8,128)S(1)} %get-tuple-element.22.own_ref.refs_4_, f32[136,128]{1,0:T(8,128)S(1)} %collective-permute-done.refs_0_.refs_5_), custom_call_target="tpu_custom_call" | custom-call | flops 2000000 | bytes 200000 | tf_op jit(solution)/shard_map/chip_total/pallas_call | solution.py:344
  5.0 3.7 %collective-permute-start.3 = (f32[136,128]{1,0:T(8,128)S(1)}, f32[136,128]{1,0:T(8,128)S(1)}, u32[]{:S(2)}, u32[]{:S(2)}) collective-permute-start(f32[136,128]{1,0:T(8,128)S(1)} %chip_total.1.own_ref.refs_0_), channel_id=1, source_target_pairs={{0,7},{1,6},{2,5},{3,4},{4,3},{5,2},{6,1},{7,0},{8,15},{9,14},{10,... | collective-permute-start | bytes 208904 | tf_op jit(solution)/shard_map/ppermute | solution.py:334
  8.6 0.4 %collective-permute-start.2 = (f32[136,128]{1,0:T(8,128)S(1)}, f32[136,128]{1,0:T(8,128)S(1)}, u32[]{:S(2)}, u32[]{:S(2)}) collective-permute-start(f32[136,128]{1,0:T(8,128)S(1)} %chip_total.1.own_ref.refs_0_), channel_id=1, source_target_pairs={{0,5},{1,4},{2,7},{3,6},{4,1},{5,0},{6,3},{7,2},{8,13},{9,12},{10,... | collective-permute-start | bytes 208904 | tf_op jit(solution)/shard_map/ppermute | solution.py:334
  9.0 0.2 %collective-permute-start.1 = (f32[136,128]{1,0:T(8,128)S(1)}, f32[136,128]{1,0:T(8,128)S(1)}, u32[]{:S(2)}, u32[]{:S(2)}) collective-permute-start(f32[136,128]{1,0:T(8,128)S(1)} %chip_total.1.own_ref.refs_0_), channel_id=1, source_target_pairs={{0,3},{1,2},{2,1},{3,0},{4,7},{5,6},{6,5},{7,4},{8,11},{9,10},{10,... | collective-permute-start | bytes 208904 | tf_op jit(solution)/shard_map/ppermute | solution.py:334
  9.2 1.6 %local_prefix.1 = (f32[16,128,128]{2,1,0:T(8,128)S(1)}, f32[16,128]{1,0:T(8,128)S(1)}) custom-call(f32[7,144,128]{2,1,0:T(8,128)S(1)} %get-tuple-element.29.tree_ref, f32[8,64,128]{2,1,0:T(8,128)S(1)} %get-tuple-element.30.kicks_ref, f32[64,128]{1,0:T(8,128)S(1)} %get-tuple-element.31.kick_first_ref, f32[16,128]{1,0:T(8,128)S(1)} %get-tuple-element.32.shifts_ref, ...), custom_call_target="tpu_custom_call" | custom-call | flops 20000000000 | bytes 200000 | tf_op jit(solution)/shard_map/local_prefix/pallas_call | solution.py:357
  10.9 0.3 %collective-permute-done.3.refs_2_.refs_3_ = f32[136,128]{1,0:T(8,128)S(1)} collective-permute-done((f32[136,128]{1,0:T(8,128)S(1)}, f32[136,128]{1,0:T(8,128)S(1)}, u32[]{:S(2)}, u32[]{:S(2)}) %collective-permute-start.3) | collective-permute-done | bytes 69664 | tf_op jit(solution)/shard_map/ppermute | solution.py:334
  11.2 1.7 %collective-permute-done.2.refs_1_.refs_2_ = f32[136,128]{1,0:T(8,128)S(1)} collective-permute-done((f32[136,128]{1,0:T(8,128)S(1)}, f32[136,128]{1,0:T(8,128)S(1)}, u32[]{:S(2)}, u32[]{:S(2)}) %collective-permute-start.2) | collective-permute-done | bytes 69664 | tf_op jit(solution)/shard_map/ppermute | solution.py:334
  12.9 0.3 %collective-permute-done.1.refs_0_.refs_1_ = f32[136,128]{1,0:T(8,128)S(1)} collective-permute-done((f32[136,128]{1,0:T(8,128)S(1)}, f32[136,128]{1,0:T(8,128)S(1)}, u32[]{:S(2)}, u32[]{:S(2)}) %collective-permute-start.1) | collective-permute-done | bytes 69664 | tf_op jit(solution)/shard_map/ppermute | solution.py:334
  13.2 0.6 %block_reach.1 = f32[8,128]{1,0:T(8,128)S(1)} custom-call(f32[8,128]{1,0:T(8,128)S(1)} %get-tuple-element.21.first_ref, f32[136,128]{1,0:T(8,128)S(1)} %chip_total.1.own_ref.refs_0_, f32[136,128]{1,0:T(8,128)S(1)} %collective-permute-done.1.refs_0_.refs_1_, f32[136,128]{1,0:T(8,128)S(1)} %collective-permute-done.2.refs_1_.refs_2_, ...), custom_call_target="tpu_custom_call" | custom-call | flops 2000000 | bytes 200000 | tf_op jit(solution)/shard_map/block_reach/pallas_call | solution.py:384
  13.8 2.4 %collective-permute-start.4 = (f32[8,128]{1,0:T(8,128)S(1)}, f32[8,128]{1,0:T(8,128)S(1)}, u32[]{:S(2)}, u32[]{:S(2)}) collective-permute-start(f32[8,128]{1,0:T(8,128)S(1)} %block_reach.1), channel_id=1, source_target_pairs={{0,9},{1,8},{2,11},{3,10},{4,13},{5,12},{6,15},{7,14},{8,1},{9,0},... | collective-permute-start | bytes 12296 | tf_op jit(solution)/shard_map/ppermute | solution.py:334
  16.1 0.3 %block_prefix.1 = (f32[128,128]{1,0:T(8,128)S(1)}, f32[128,128]{1,0:T(8,128)S(1)}, f32[8,128]{1,0:T(8,128)S(1)}) custom-call(f32[16,128]{1,0:T(8,128)S(1)} %get-tuple-element.23.guess_ref, f32[136,128]{1,0:T(8,128)S(1)} %chip_total.1.own_ref.refs_0_, f32[136,128]{1,0:T(8,128)S(1)} %collective-permute-done.1.refs_0_.refs_1_, ...), custom_call_target="tpu_custom_call" | custom-call | flops 2000000000 | bytes 200000 | tf_op jit(solution)/shard_map/block_prefix/pallas_call | solution.py:416
  16.5 1.2 %collective-permute-done.4.arrived_ref = f32[8,128]{1,0:T(8,128)S(1)} collective-permute-done((f32[8,128]{1,0:T(8,128)S(1)}, f32[8,128]{1,0:T(8,128)S(1)}, u32[]{:S(2)}, u32[]{:S(2)}) %collective-permute-start.4) | collective-permute-done | bytes 4128 | tf_op jit(solution)/shard_map/ppermute | solution.py:334
  17.7 0.8 %finish.1 = f32[16,128]{1,0:T(8,128)} custom-call(f32[8,128]{1,0:T(8,128)S(1)} %collective-permute-done.4.arrived_ref, f32[8,128]{1,0:T(8,128)S(1)} %get-tuple-element.21.first_ref, f32[128,128]{1,0:T(8,128)S(1)} %get-tuple-element.24.ahead_ref, f32[128,128]{1,0:T(8,128)S(1)} %get-tuple-element.25.shift_ref, f32[8,128]{1,0:T(8,128)S(1)} %get-tuple-element.26.origin_ref, ...), custom_call_target="tpu_custom_call" | custom-call | flops 2000000 | bytes 200000 | tf_op jit(solution)/shard_map/finish/pallas_call | solution.py:423
Async XLA Ops:
  3.3 1.5 %collective-permute-start = (f32[136,128]{1,0:T(8,128)S(1)}, f32[136,128]{1,0:T(8,128)S(1)}, u32[]{:S(2)}, u32[]{:S(2)}) collective-permute-start(f32[136,128]{1,0:T(8,128)S(1)} %get-tuple-element.22.own_ref.refs_4_), channel_id=1, source_target_pairs={{0,1},{1,0},{2,3},{3,2},{4,5},{5,4},{6,7},{7,6},{8,9},{9,8},{10,11... | collective-permute-start | bytes 208904 | tf_op jit(solution)/shard_map/ppermute | solution.py:334
  5.0 6.2 %collective-permute-start.3 = (f32[136,128]{1,0:T(8,128)S(1)}, f32[136,128]{1,0:T(8,128)S(1)}, u32[]{:S(2)}, u32[]{:S(2)}) collective-permute-start(f32[136,128]{1,0:T(8,128)S(1)} %chip_total.1.own_ref.refs_0_), channel_id=1, source_target_pairs={{0,7},{1,6},{2,5},{3,4},{4,3},{5,2},{6,1},{7,0},{8,15},{9,14},{10,... | collective-permute-start | bytes 208904 | tf_op jit(solution)/shard_map/ppermute | solution.py:334
  8.6 4.3 %collective-permute-start.2 = (f32[136,128]{1,0:T(8,128)S(1)}, f32[136,128]{1,0:T(8,128)S(1)}, u32[]{:S(2)}, u32[]{:S(2)}) collective-permute-start(f32[136,128]{1,0:T(8,128)S(1)} %chip_total.1.own_ref.refs_0_), channel_id=1, source_target_pairs={{0,5},{1,4},{2,7},{3,6},{4,1},{5,0},{6,3},{7,2},{8,13},{9,12},{10,... | collective-permute-start | bytes 208904 | tf_op jit(solution)/shard_map/ppermute | solution.py:334
  9.0 4.1 %collective-permute-start.1 = (f32[136,128]{1,0:T(8,128)S(1)}, f32[136,128]{1,0:T(8,128)S(1)}, u32[]{:S(2)}, u32[]{:S(2)}) collective-permute-start(f32[136,128]{1,0:T(8,128)S(1)} %chip_total.1.own_ref.refs_0_), channel_id=1, source_target_pairs={{0,3},{1,2},{2,1},{3,0},{4,7},{5,6},{6,5},{7,4},{8,11},{9,10},{10,... | collective-permute-start | bytes 208904 | tf_op jit(solution)/shard_map/ppermute | solution.py:334
  13.8 4.0 %collective-permute-start.4 = (f32[8,128]{1,0:T(8,128)S(1)}, f32[8,128]{1,0:T(8,128)S(1)}, u32[]{:S(2)}, u32[]{:S(2)}) collective-permute-start(f32[8,128]{1,0:T(8,128)S(1)} %block_reach.1), channel_id=1, source_target_pairs={{0,9},{1,8},{2,11},{3,10},{4,13},{5,12},{6,15},{7,14},{8,1},{9,0},... | collective-permute-start | bytes 12296 | tf_op jit(solution)/shard_map/ppermute | solution.py:334

commit v4 on v3

--- a/solution.py
+++ b/solution.py
@@ -55,40 +55,69 @@
     width = state // 2
     h = step_size
     guess = guess_ref[...]
+    hidden = weight_ref.shape[1]
     points = jnp.concatenate([guess, jnp.broadcast_to(start_ref[...], (8, state))], axis=0)
     weight = weight_ref[...]
-    weight2 = split(weight)
+    weight_high, weight_low = split(weight)
+    wide = jnp.concatenate([weight_high, weight_high, weight_low, jnp.zeros_like(weight_low)], axis=0)
+    double_high = jnp.concatenate([weight_high, weight_high], axis=0)
+    double = jnp.concatenate([double_high, weight_low, weight_low], axis=0)
     bias, amp = bias_ref[...], amp_ref[...]
-    coords, momenta = points[:, :width], points[:, width:]
-
-    def forces(at):
-        gate = jax.nn.sigmoid(dot3(split(at), weight2) + bias)
-        scaled = amp * gate
-        grad = dot3(split(scaled), weight2, NT) + curvature * at
-        return grad, scaled * (1.0 - gate)
-
-    grad_zero, curve_zero = forces(coords)
-    half = momenta - 0.5 * h * grad_zero
+
+    def side(value):
+        return lax.broadcasted_iota(jnp.int32, value.shape, 1) >= width
+
+    def swap(value):
+        return jnp.concatenate([value[:, width:], value[:, :width]], axis=1)
+
+    def stack_left(twice):
+        high, low = split(twice)
+        mixed = jnp.where(side(twice), twice - high.astype(jnp.float32), high.astype(jnp.float32))
+        return jnp.concatenate([mixed.astype(jnp.bfloat16), high], axis=1)
+
+    def stack_right(value):
+        high, low = split(value)
+        return jnp.concatenate([high, high, low, jnp.zeros_like(low)], axis=0)
+
+    def to_hidden(twice):
+        return jnp.dot(stack_left(twice), wide, preferred_element_type=jnp.float32)
+
+    def from_hidden(value):
+        high, low = split(value)
+        both = lax.dot_general(high, double, NT, preferred_element_type=jnp.float32)
+        small = lax.dot_general(low, double_high, NT, preferred_element_type=jnp.float32)
+        return both[:, :state] + (both[:, state:] + small)
+
+    swapped = swap(points)
+    right = side(points)
+    coords = jnp.where(right, swapped, points)
+    momenta = jnp.where(right, points, swapped)
+    gate = jax.nn.sigmoid(to_hidden(coords) + bias)
+    scaled = amp * gate
+    curve_zero = scaled * (1.0 - gate)
+    half = momenta - 0.5 * h * (from_hidden(scaled) + curvature * coords)
     moved = coords + h * half
-    grad_one, curve_one = forces(moved)
-    landed = half - 0.5 * h * grad_one
-    image = jnp.concatenate([moved, landed], axis=1)
+
+    pushed = moved[:rows] - jnp.concatenate([coords[1:rows], coords[:1]], axis=0)
+    curve_next = jnp.concatenate([curve_zero[1:rows], jnp.zeros((1, hidden), jnp.float32)], axis=0)
+    spread_out = to_hidden(jnp.concatenate([moved, pushed], axis=0))
+    count = points.shape[0]
+    gate = jax.nn.sigmoid(spread_out[:count] + bias)
+    scaled = amp * gate
+    curve_one = scaled * (1.0 - gate)
+    gathered = from_hidden(jnp.concatenate([scaled, spread_out[count:] * curve_next], axis=0))
+    landed = half - 0.5 * h * (gathered[:count] + curvature * moved)
+    image = jnp.where(right, landed, moved)
     first_ref[...] = image[rows:]
-
-    residual = image[:rows - 1] - guess[1:]
-    residual = jnp.concatenate([residual, jnp.zeros((1, state), jnp.float32)], axis=0)
-    curve_next = jnp.concatenate([curve_zero[1:rows], jnp.zeros((1, curve_zero.shape[1]), jnp.float32)], axis=0)
-    pushed = residual[:, :width]
-    inner = dot3(split(pushed), weight2) * curve_next
-    kicked = 0.5 * h * (dot3(split(inner), weight2, NT) + curvature * pushed)
-    shifts = jnp.concatenate([pushed, residual[:, width:] - kicked], axis=1)
+    kicked = 0.5 * h * (gathered[count:] + curvature * pushed)
+    residual = image[:rows] - jnp.concatenate([guess[1:], guess[:1]], axis=0)
+    shifts = residual - jnp.where(right[:rows], kicked, 0.0)
     row_id = lax.broadcasted_iota(jnp.int32, (rows, state), 0)
     shifts = jnp.where(row_id == rows - 1, image[:rows], shifts)
     shifts_ref[...] = shifts
     curve_ref[...] = curve_zero[:rows]
-
-    double = jnp.concatenate([weight, weight], axis=0)
-    double2 = split(double)
+    drifted = shifts + jnp.where(right[:rows], 0.0, h * swap(shifts))
+
     line = lax.broadcasted_iota(jnp.int32, (width, state), 0)
     lane = lax.broadcasted_iota(jnp.int32, (width, state), 1)
     unit2 = jnp.where((lane == line) | (lane == line + width), 1.0, 0.0)
@@ -96,14 +125,13 @@
     unit_top = jnp.where(lane == line, 1.0, 0.0)
     unit_low = jnp.where(lane == line + width, 1.0, 0.0)
     between = (curve_one[:rows] + curve_next) * (0.5 * h)
-
     rows_of_kick = [curve_zero[0:1] * (0.5 * h)] + [between[j:j + 1] for j in range(rows)]
     for j, weights_row in enumerate(rows_of_kick):
         scaled_high, scaled_low = split(weight * weights_row)
         high_ref[j * width:(j + 1) * width] = scaled_high
         low_ref[j * width:(j + 1) * width] = scaled_low
-    product = lax.dot_general(high_ref[...], jnp.concatenate(double2, axis=0), NT, preferred_element_type=jnp.float32)
-    small = lax.dot_general(low_ref[...], double2[0], NT, preferred_element_type=jnp.float32)
+    product = lax.dot_general(high_ref[...], double, NT, preferred_element_type=jnp.float32)
+    small = lax.dot_general(low_ref[...], double_high, NT, preferred_element_type=jnp.float32)
     product = product[:, :state] + (product[:, state:] + small)
     kicks = [
         product[j * width:(j + 1) * width] + (0.5 * h * curvature * (1 if j in (0, rows) else 2)) * unit2
@@ -114,20 +142,17 @@
     for j in range(0, rows, 2):
         kicks_ref[j // 2] = kicks[j]
 
-    rolled = jnp.concatenate([shifts[:, width:], shifts[:, :width]], axis=1)
-    lane_rows = lax.broadcasted_iota(jnp.int32, (rows, state), 1)
-    drifted = shifts + jnp.where(lane_rows < width, h * rolled, 0.0)
     level = []
+    drifted_twice = jnp.where(side(drifted), swap(drifted), drifted)
     for k in range(rows // 2):
         a, b = kicks[2 * k], kicks[2 * k + 1]
-        moved_row = jnp.broadcast_to(drifted[2 * k:2 * k + 1, :width], (PAD, width))
-        left = jnp.concatenate([a[:, :width], moved_row], axis=0)
-        both = dot3(split(left), split(b))
+        moved_row = jnp.broadcast_to(drifted_twice[2 * k:2 * k + 1], (PAD, state))
+        both = jnp.dot(stack_left(jnp.concatenate([a, moved_row], axis=0)), stack_right(b), preferred_element_type=jnp.float32)
         prod = both[:width]
         top = unit_top - jnp.where(right, a + b - h * prod, h * a)
         low = 2 * h * unit_top + unit_low - jnp.where(right, h * a + 2 * h * b - (h * h) * prod, (h * h) * a)
         if k == 0:
-            top = top - dot3(split(kick_first[:, :width]), split(low))
+            top = top - jnp.dot(stack_left(kick_first), stack_right(low), preferred_element_type=jnp.float32)
         tail = drifted[2 * k:2 * k + 1] - jnp.where(right[:PAD], both[width:], 0.0) + shifts[2 * k + 1:2 * k + 2]
         level.append(jnp.concatenate([top, low, tail], axis=0))
     slot = 0
@@ -181,9 +206,18 @@
 def reach_kernel(source, axis_place, count, first_ref, own_ref, *refs):
     others, (out_ref, stack_ref) = refs[:count - 1], refs[count - 1:]
     ordered(own_ref, others, stack_ref, axis_place(), source)
-    state = first_ref[...]
-    for position in range(count):
-        state = apply(state, stack_ref[position])
+    size = first_ref.shape[1]
+    state = first_ref[0:1]
+    for position in range(0, count - 1, 2):
+        matrix_a, shift_a, origin_a = spread(stack_ref[position], size)
+        matrix_b, shift_b, origin_b = spread(stack_ref[position + 1], size)
+        turned = jnp.sum(matrix_a.T * (state - origin_a), axis=1, keepdims=True)
+        column = jnp.broadcast_to(shift_a - origin_b, (size, size)).T
+        state = jnp.sum(matrix_b * turned, axis=0, keepdims=True) + (
+            jnp.sum(matrix_b * column, axis=0, keepdims=True) + shift_b)
+    state = jnp.broadcast_to(state, (8, size))
+    if count % 2:
+        state = apply(state, stack_ref[count - 1])
     out_ref[...] = state
 
 

time: 18.7 us -> 17.9 us (0.957)
  Pallas kernels: 6.82 us -> 6 us
    pallas_call x1, Pallas kernels: 3.27 us -> 2.64 us  [shards(): call(local_kernel, [packed, f32((8, size)), f32((nodes, size + PAD, size)...]
    pallas_call x1, Pallas kernels: 0.58 us -> 0.38 us  [shards(): call(functools.partial(reach_kernel, group_source, group_place, group), f...]
where the time goes in v4:
time: 17.9 us; the launch traced here: 17.7 us
  starting transfers between devices  7.25 us (41%)
  Pallas kernels  6 us (34%)
  waiting for transfers between devices  4.44 us (25%)
    ppermute x5, starting transfers between devices, exchange(): return lax.ppermute(value, axes, pairs)  7.25 us
    ppermute x5, waiting for transfers between devices, exchange(): return lax.ppermute(value, axes, pairs)  4.44 us
    pallas_call x1, Pallas kernels, shards(): call(local_kernel, [packed, f32((8, size)), f32((nodes, size + PAD, size)...  2.64 us
    pallas_call x1, Pallas kernels, shards(): call(prefix_kernel, [f32((rows, size, size)), f32((rows, size))], [pltpu....  1.63 us
    pallas_call x1, Pallas kernels, shards(): call(functools.partial(finish_kernel, later_block), f32((rows, size)), na...  0.78 us
    pallas_call x1, Pallas kernels, shards(): call(functools.partial(reach_kernel, group_source, group_place, group), f...  0.38 us
  transfers between devices with their start and end apart: 5, of which 5 were waited for; matrix products, arithmetic and copies ran while one was open for 0% of the time, Pallas kernels for 11%

profile of v4, /device:TPU:0, one launch (start us, length us, event | category | flops | bytes accessed | tf_op | source)
XLA Modules:
  0.0 17.7 jit_solution(13559341659153004377)
XLA Ops:
  0.0 2.6 %local_maps.1 = (f32[136,128]{1,0:T(8,128)S(1)}, f32[8,128]{1,0:T(8,128)S(1)}, f32[7,144,128]{2,1,0:T(8,128)S(1)}, f32[8,64,128]{2,1,0:T(8,128)S(1)}, f32[64,128...) custom-call(f32[16,128]{1,0:T(8,128)} %guess_in.1, ...), custom_call_target="tpu_custom_call" | custom-call | flops 100000000 | bytes 200000 | tf_op jit(solution)/shard_map/local_maps/pallas_call | solution.py:356
  2.6 0.6 %collective-permute-start = (f32[136,128]{1,0:T(8,128)S(1)}, f32[136,128]{1,0:T(8,128)S(1)}, u32[]{:S(2)}, u32[]{:S(2)}) collective-permute-start(f32[136,128]{1,0:T(8,128)S(1)} %get-tuple-element.22.own_ref.refs_4_), channel_id=1, source_target_pairs={{0,1},{1,0},{2,3},{3,2},{4,5},{5,4},{6,7},{7,6},{8,9},{9,8},{10,11... | collective-permute-start | bytes 208904 | tf_op jit(solution)/shard_map/ppermute | solution.py:368
  3.2 0.9 %collective-permute-done.refs_0_.refs_5_ = f32[136,128]{1,0:T(8,128)S(1)} collective-permute-done((f32[136,128]{1,0:T(8,128)S(1)}, f32[136,128]{1,0:T(8,128)S(1)}, u32[]{:S(2)}, u32[]{:S(2)}) %collective-permute-start) | collective-permute-done | bytes 69664 | tf_op jit(solution)/shard_map/ppermute | solution.py:368
  4.1 0.2 %chip_total.1.own_ref.refs_0_ = f32[136,128]{1,0:T(8,128)S(1)} custom-call(f32[136,128]{1,0:T(8,128)S(1)} %get-tuple-element.22.own_ref.refs_4_, f32[136,128]{1,0:T(8,128)S(1)} %collective-permute-done.refs_0_.refs_5_), custom_call_target="tpu_custom_call" | custom-call | flops 2000000 | bytes 200000 | tf_op jit(solution)/shard_map/chip_total/pallas_call | solution.py:378
  4.3 3.7 %collective-permute-start.3 = (f32[136,128]{1,0:T(8,128)S(1)}, f32[136,128]{1,0:T(8,128)S(1)}, u32[]{:S(2)}, u32[]{:S(2)}) collective-permute-start(f32[136,128]{1,0:T(8,128)S(1)} %chip_total.1.own_ref.refs_0_), channel_id=1, source_target_pairs={{0,7},{1,6},{2,5},{3,4},{4,3},{5,2},{6,1},{7,0},{8,15},{9,14},{10,... | collective-permute-start | bytes 208904 | tf_op jit(solution)/shard_map/ppermute | solution.py:368
  8.0 0.4 %collective-permute-start.2 = (f32[136,128]{1,0:T(8,128)S(1)}, f32[136,128]{1,0:T(8,128)S(1)}, u32[]{:S(2)}, u32[]{:S(2)}) collective-permute-start(f32[136,128]{1,0:T(8,128)S(1)} %chip_total.1.own_ref.refs_0_), channel_id=1, source_target_pairs={{0,5},{1,4},{2,7},{3,6},{4,1},{5,0},{6,3},{7,2},{8,13},{9,12},{10,... | collective-permute-start | bytes 208904 | tf_op jit(solution)/shard_map/ppermute | solution.py:368
  8.4 0.2 %collective-permute-start.1 = (f32[136,128]{1,0:T(8,128)S(1)}, f32[136,128]{1,0:T(8,128)S(1)}, u32[]{:S(2)}, u32[]{:S(2)}) collective-permute-start(f32[136,128]{1,0:T(8,128)S(1)} %chip_total.1.own_ref.refs_0_), channel_id=1, source_target_pairs={{0,3},{1,2},{2,1},{3,0},{4,7},{5,6},{6,5},{7,4},{8,11},{9,10},{10,... | collective-permute-start | bytes 208904 | tf_op jit(solution)/shard_map/ppermute | solution.py:368
  8.6 1.6 %local_prefix.1 = (f32[16,128,128]{2,1,0:T(8,128)S(1)}, f32[16,128]{1,0:T(8,128)S(1)}) custom-call(f32[7,144,128]{2,1,0:T(8,128)S(1)} %get-tuple-element.29.tree_ref, f32[8,64,128]{2,1,0:T(8,128)S(1)} %get-tuple-element.30.kicks_ref, f32[64,128]{1,0:T(8,128)S(1)} %get-tuple-element.31.kick_first_ref, f32[16,128]{1,0:T(8,128)S(1)} %get-tuple-element.32.shifts_ref, ...), custom_call_target="tpu_custom_call" | custom-call | flops 20000000000 | bytes 200000 | tf_op jit(solution)/shard_map/local_prefix/pallas_call | solution.py:391
  10.2 0.3 %collective-permute-done.3.refs_2_.refs_3_ = f32[136,128]{1,0:T(8,128)S(1)} collective-permute-done((f32[136,128]{1,0:T(8,128)S(1)}, f32[136,128]{1,0:T(8,128)S(1)}, u32[]{:S(2)}, u32[]{:S(2)}) %collective-permute-start.3) | collective-permute-done | bytes 69664 | tf_op jit(solution)/shard_map/ppermute | solution.py:368
  10.6 1.7 %collective-permute-done.2.refs_1_.refs_2_ = f32[136,128]{1,0:T(8,128)S(1)} collective-permute-done((f32[136,128]{1,0:T(8,128)S(1)}, f32[136,128]{1,0:T(8,128)S(1)}, u32[]{:S(2)}, u32[]{:S(2)}) %collective-permute-start.2) | collective-permute-done | bytes 69664 | tf_op jit(solution)/shard_map/ppermute | solution.py:368
  12.3 0.3 %collective-permute-done.1.refs_0_.refs_1_ = f32[136,128]{1,0:T(8,128)S(1)} collective-permute-done((f32[136,128]{1,0:T(8,128)S(1)}, f32[136,128]{1,0:T(8,128)S(1)}, u32[]{:S(2)}, u32[]{:S(2)}) %collective-permute-start.1) | collective-permute-done | bytes 69664 | tf_op jit(solution)/shard_map/ppermute | solution.py:368
  12.6 0.4 %block_reach.1 = f32[8,128]{1,0:T(8,128)S(1)} custom-call(f32[8,128]{1,0:T(8,128)S(1)} %get-tuple-element.21.first_ref, f32[136,128]{1,0:T(8,128)S(1)} %chip_total.1.own_ref.refs_0_, f32[136,128]{1,0:T(8,128)S(1)} %collective-permute-done.1.refs_0_.refs_1_, f32[136,128]{1,0:T(8,128)S(1)} %collective-permute-done.2.refs_1_.refs_2_, ...), custom_call_target="tpu_custom_call" | custom-call | flops 2000000 | bytes 200000 | tf_op jit(solution)/shard_map/block_reach/pallas_call | solution.py:418
  13.0 2.4 %collective-permute-start.4 = (f32[8,128]{1,0:T(8,128)S(1)}, f32[8,128]{1,0:T(8,128)S(1)}, u32[]{:S(2)}, u32[]{:S(2)}) collective-permute-start(f32[8,128]{1,0:T(8,128)S(1)} %block_reach.1), channel_id=1, source_target_pairs={{0,9},{1,8},{2,11},{3,10},{4,13},{5,12},{6,15},{7,14},{8,1},{9,0},... | collective-permute-start | bytes 12296 | tf_op jit(solution)/shard_map/ppermute | solution.py:368
  15.4 0.3 %block_prefix.1 = (f32[128,128]{1,0:T(8,128)S(1)}, f32[128,128]{1,0:T(8,128)S(1)}, f32[8,128]{1,0:T(8,128)S(1)}) custom-call(f32[16,128]{1,0:T(8,128)S(1)} %get-tuple-element.23.guess_ref, f32[136,128]{1,0:T(8,128)S(1)} %chip_total.1.own_ref.refs_0_, f32[136,128]{1,0:T(8,128)S(1)} %collective-permute-done.1.refs_0_.refs_1_, ...), custom_call_target="tpu_custom_call" | custom-call | flops 2000000000 | bytes 200000 | tf_op jit(solution)/shard_map/block_prefix/pallas_call | solution.py:450
  15.7 1.2 %collective-permute-done.4.arrived_ref = f32[8,128]{1,0:T(8,128)S(1)} collective-permute-done((f32[8,128]{1,0:T(8,128)S(1)}, f32[8,128]{1,0:T(8,128)S(1)}, u32[]{:S(2)}, u32[]{:S(2)}) %collective-permute-start.4) | collective-permute-done | bytes 4128 | tf_op jit(solution)/shard_map/ppermute | solution.py:368
  17.0 0.8 %finish.1 = f32[16,128]{1,0:T(8,128)} custom-call(f32[8,128]{1,0:T(8,128)S(1)} %collective-permute-done.4.arrived_ref, f32[8,128]{1,0:T(8,128)S(1)} %get-tuple-element.21.first_ref, f32[128,128]{1,0:T(8,128)S(1)} %get-tuple-element.24.ahead_ref, f32[128,128]{1,0:T(8,128)S(1)} %get-tuple-element.25.shift_ref, f32[8,128]{1,0:T(8,128)S(1)} %get-tuple-element.26.origin_ref, ...), custom_call_target="tpu_custom_call" | custom-call | flops 2000000 | bytes 200000 | tf_op jit(solution)/shard_map/finish/pallas_call | solution.py:457
Async XLA Ops:
  2.6 1.5 %collective-permute-start = (f32[136,128]{1,0:T(8,128)S(1)}, f32[136,128]{1,0:T(8,128)S(1)}, u32[]{:S(2)}, u32[]{:S(2)}) collective-permute-start(f32[136,128]{1,0:T(8,128)S(1)} %get-tuple-element.22.own_ref.refs_4_), channel_id=1, source_target_pairs={{0,1},{1,0},{2,3},{3,2},{4,5},{5,4},{6,7},{7,6},{8,9},{9,8},{10,11... | collective-permute-start | bytes 208904 | tf_op jit(solution)/shard_map/ppermute | solution.py:368
  4.3 6.2 %collective-permute-start.3 = (f32[136,128]{1,0:T(8,128)S(1)}, f32[136,128]{1,0:T(8,128)S(1)}, u32[]{:S(2)}, u32[]{:S(2)}) collective-permute-start(f32[136,128]{1,0:T(8,128)S(1)} %chip_total.1.own_ref.refs_0_), channel_id=1, source_target_pairs={{0,7},{1,6},{2,5},{3,4},{4,3},{5,2},{6,1},{7,0},{8,15},{9,14},{10,... | collective-permute-start | bytes 208904 | tf_op jit(solution)/shard_map/ppermute | solution.py:368
  8.0 4.2 %collective-permute-start.2 = (f32[136,128]{1,0:T(8,128)S(1)}, f32[136,128]{1,0:T(8,128)S(1)}, u32[]{:S(2)}, u32[]{:S(2)}) collective-permute-start(f32[136,128]{1,0:T(8,128)S(1)} %chip_total.1.own_ref.refs_0_), channel_id=1, source_target_pairs={{0,5},{1,4},{2,7},{3,6},{4,1},{5,0},{6,3},{7,2},{8,13},{9,12},{10,... | collective-permute-start | bytes 208904 | tf_op jit(solution)/shard_map/ppermute | solution.py:368
  8.4 4.1 %collective-permute-start.1 = (f32[136,128]{1,0:T(8,128)S(1)}, f32[136,128]{1,0:T(8,128)S(1)}, u32[]{:S(2)}, u32[]{:S(2)}) collective-permute-start(f32[136,128]{1,0:T(8,128)S(1)} %chip_total.1.own_ref.refs_0_), channel_id=1, source_target_pairs={{0,3},{1,2},{2,1},{3,0},{4,7},{5,6},{6,5},{7,4},{8,11},{9,10},{10,... | collective-permute-start | bytes 208904 | tf_op jit(solution)/shard_map/ppermute | solution.py:368
  13.0 4.0 %collective-permute-start.4 = (f32[8,128]{1,0:T(8,128)S(1)}, f32[8,128]{1,0:T(8,128)S(1)}, u32[]{:S(2)}, u32[]{:S(2)}) collective-permute-start(f32[8,128]{1,0:T(8,128)S(1)} %block_reach.1), channel_id=1, source_target_pairs={{0,9},{1,8},{2,11},{3,10},{4,13},{5,12},{6,15},{7,14},{8,1},{9,0},... | collective-permute-start | bytes 12296 | tf_op jit(solution)/shard_map/ppermute | solution.py:368
